TPU v7x, 32 devices: a whole 2x2x4 slice. The times are simulated.
32 devices in a mesh: row: 8 (over z, core), col: 4 (over y, x).
Axes of the slice: x: 2, y: 2, z: 4, core: 2. Of those that a mesh axis runs over, the one named last changes fastest.
Arguments:
- x_fwd: bfloat16 [512, 6144], P('row', 'col'), may hold values from -6 to 6
- x_bwd: bfloat16 [512, 6144], P('row', 'col'), may hold values from -6 to 6
- grad_out: bfloat16 [512, 6144], P('row', 'col'), may hold values from -1.5 to 1.5
- gain: float32 [6144], P('col'), may hold values from 0.1 to 1.9
- w_up: bfloat16 [6144, 12288], P('col', 'row'), may hold values from -0.078125 to 0.078125
- w_down: bfloat16 [12288, 6144], P('row', 'col'), may hold values from -0.0546875 to 0.0546875
Outputs:
- y_fwd: bfloat16 [512, 6144], P('row', 'col')
- dx_bwd: bfloat16 [512, 6144], P('row', 'col')
- step_up: float32 [6144, 12288], P('col', 'row')
- step_down: float32 [12288, 6144], P('row', 'col')
- step_gain: float32 [6144], P('col')
- grad_rms: float32 [], replicated
All inputs are finite; a program needn't handle non-finite values.
Results may differ from a plain program's by a relative error of at most 0.0017.
The roundings to bfloat16 on the way count: a program that leaves them out, or rounds other values in their place, can miss the bound.
Values may be sent and summed in bfloat16 or wider, within the bound.
A program may use at most 128 MiB of HBM per device.

v0:
```python
import functools
import math

import jax
import jax.numpy as jnp
from jax import lax
from jax.experimental import pallas as pl
from jax.experimental.pallas import tpu as pltpu
from jax.sharding import PartitionSpec as P

D = 6144
FF = 12288


eps = 1e-06
clip_share = 0.25


def erf_gelu(value):
    return 0.5 * value * (1.0 + lax.erf(value * 0.7071067811865476))


def gelu_slope(value):
    return (
        0.5 * (1.0 + lax.erf(value * 0.7071067811865476))
        + value * jnp.exp(-0.5 * value * value) * 0.3989422804014327
    )


def contract(left, right, left_dim, right_dim):
    return lax.dot_general(
        left, right, (((left_dim,), (right_dim,)), ((), ())), preferred_element_type=jnp.float32
    )


def row_sums(tokens):
    values = tokens.astype(jnp.float32)
    return (jnp.sum(values, -1), jnp.sum(values * values, -1))


def normalize(tokens, first, second):
    values = tokens.astype(jnp.float32)
    centre = first / D
    spread = second / D - centre * centre
    inv_scale = lax.rsqrt(spread + eps)
    return ((values - centre[:, None]) * inv_scale[:, None], inv_scale)


def up_both(normed_a, normed_b, w_up):
    full_a, full_b = (
        lax.all_gather(normed_a, "row", axis=0, tiled=True),
        lax.all_gather(normed_b, "row", axis=0, tiled=True),
    )
    width = w_up.shape[1]
    summed = lax.psum_scatter(
        jnp.concatenate(
            [
                jnp.dot(full_a, w_up, preferred_element_type=jnp.float32),
                jnp.dot(full_b, w_up, preferred_element_type=jnp.float32),
            ],
            1,
        ),
        "col",
        scatter_dimension=0,
        tiled=True,
    )
    return (summed[:, :width], summed[:, width:], full_b)


def on_device(x_fwd, x_bwd, grad_out, gain, w_up, w_down):
    first_a, second_a = row_sums(x_fwd)
    first_b, second_b = row_sums(x_bwd)
    first_a, second_a, first_b, second_b = lax.psum((first_a, second_a, first_b, second_b), "col")
    centred_a, _ = normalize(x_fwd, first_a, second_a)
    centred_b, inv_scale = normalize(x_bwd, first_b, second_b)
    normed_a = (centred_a * gain).astype(jnp.bfloat16)
    normed_b = (centred_b * gain).astype(jnp.bfloat16)
    pre_a, pre_b, normed_full = up_both(normed_a, normed_b, w_up)
    hidden_a = erf_gelu(pre_a).astype(jnp.bfloat16)
    output_part = jnp.dot(
        lax.all_gather(hidden_a, "col", axis=0, tiled=True),
        w_down,
        preferred_element_type=jnp.float32,
    )
    output_sum = lax.psum_scatter(output_part, "row", scatter_dimension=0, tiled=True)
    y_fwd = (x_fwd.astype(jnp.float32) + output_sum).astype(jnp.bfloat16)
    hidden_b = erf_gelu(pre_b).astype(jnp.bfloat16)
    grad_full = lax.all_gather(grad_out, "row", axis=0, tiled=True)
    grad_hidden = lax.psum_scatter(
        contract(grad_full, w_down, 1, 1), "col", scatter_dimension=0, tiled=True
    )
    grad_pre = (grad_hidden * gelu_slope(pre_b)).astype(jnp.bfloat16)
    hidden_piece = lax.all_gather(hidden_b, "col", axis=0, tiled=True)
    pre_piece = lax.all_gather(grad_pre, "col", axis=0, tiled=True)
    down_total = contract(hidden_piece, grad_full, 0, 0)
    up_total = contract(normed_full, pre_piece, 0, 0)
    input_total = contract(pre_piece, w_up, 1, 1)
    grad_normed = lax.psum_scatter(input_total, "row", scatter_dimension=0, tiled=True)
    scaled = grad_normed * gain
    first_back = jnp.sum(scaled, -1)
    second_back = jnp.sum(scaled * centred_b, -1)
    first_back, second_back = lax.psum((first_back, second_back), "col")
    dx_bwd = (
        grad_out.astype(jnp.float32)
        + inv_scale[:, None]
        * (scaled - first_back[:, None] / D - centred_b * (second_back[:, None] / D))
    ).astype(jnp.bfloat16)
    gain_part = jnp.sum(grad_normed * centred_b, 0)
    weight_squares = jnp.sum(up_total * up_total) + jnp.sum(down_total * down_total)
    g_gain = lax.psum(gain_part, "row")
    first_row = (lax.axis_index("row") == 0).astype(jnp.float32)
    total = lax.psum(weight_squares + first_row * jnp.sum(g_gain * g_gain), ("row", "col"))
    param_count = 2 * D * FF + D
    norm_value = jnp.sqrt(total)
    grad_rms = norm_value / math.sqrt(param_count)
    factor = jnp.minimum(1.0, clip_share * math.sqrt(param_count) / norm_value)
    return (y_fwd, dx_bwd, up_total * factor, down_total * factor, g_gain * factor, grad_rms)


MESH = pl.DeviceIdType.MESH
VMEM = pl.BlockSpec(memory_space=pltpu.VMEM)
F32 = jnp.float32
BF16 = jnp.bfloat16
DMA = pltpu.SemaphoreType.DMA
GRANT = 60 * 1024 * 1024


def greet(peers):
    barrier = pltpu.get_barrier_semaphore()
    for peer in peers:
        pl.semaphore_signal(barrier, inc=1, device_id=peer, device_id_type=MESH)
    pl.semaphore_wait(barrier, len(peers))


def send(src, dst, send_sem, recv_sem, peer):
    return pltpu.make_async_remote_copy(
        src_ref=src, dst_ref=dst, send_sem=send_sem, recv_sem=recv_sem,
        device_id=peer, device_id_type=MESH,
    )


def arrived(ref, sem, peer):
    pltpu.make_async_remote_copy(
        src_ref=ref, dst_ref=ref, send_sem=sem, recv_sem=sem,
        device_id=peer, device_id_type=MESH,
    ).wait_recv()


def greet_line(line, chip, chips, others):
    barrier = pltpu.get_barrier_semaphore()
    for peer in others:
        pl.semaphore_signal(barrier, inc=1, device_id=peer, device_id_type=MESH)

    @pl.when(chip > 0)
    def _():
        pl.semaphore_signal(barrier, inc=1, device_id=line(-1), device_id_type=MESH)

    @pl.when(chip < chips - 1)
    def _():
        pl.semaphore_signal(barrier, inc=1, device_id=line(1), device_id_type=MESH)

    beside = jnp.minimum(chip, 1) + jnp.minimum(chips - 1 - chip, 1)
    pl.semaphore_wait(barrier, len(others) + beside)


def normal_of(values, stats, at, width):
    centre = stats[:, at : at + 1] / width
    spread = stats[:, at + 1 : at + 2] / width - centre * centre
    inv = lax.rsqrt(spread + eps)
    return (values - centre) * inv, inv


def lanes_of(columns):
    rows = columns[0].shape[0]
    lane = lax.broadcasted_iota(jnp.int32, (rows, 128), 1)
    out = jnp.zeros((rows, 128), F32)
    for i, column in enumerate(columns):
        out = jnp.where(lane == i, column, out)
    return out


def layer_kernel(R, C, width, xa, xb, go, gain, w_up_hbm, w_down_hbm, full, stats, acts, sums,
                 w_up, w_down, st_own, st_in, out_send, buf, inb, own,
                 part, from_sib, from_left, from_right,
                 w_sem, st_send, st_recv, s_right, s_left, s_sib, recv, sem_s, sem_r, g_s, g_r,
                 sib_s, sib_r, right_s, left_s, left_r, right_r):
    row, col = lax.axis_index("row"), lax.axis_index("col")
    chips = R // 2
    chip, core = row // 2, row % 2
    sib = {"row": row + 1 - 2 * core, "col": col}

    def line(step):
        return {"row": row + 2 * step, "col": col}

    cols = [{"row": row, "col": (col + i) % C} for i in range(1, C)]
    flip_x = col + 1 - 2 * (col % 2)
    flip_y = (col + 2) % 4
    diag = 3 - col
    peer_x, peer_y = {"row": row, "col": flip_x}, {"row": row, "col": flip_y}
    share = xa.shape[0]
    tokens, wide = out_send.shape[1], out_send.shape[2]
    half = wide // 2
    tile = half // 2
    load_up = pltpu.make_async_copy(w_up_hbm, w_up, w_sem.at[0])
    load_down = pltpu.make_async_copy(w_down_hbm, w_down, w_sem.at[1])
    load_down.start()
    load_up.start()
    greet_line(line, chip, chips, cols + [sib])

    def block(j, owner):
        return full.at[j, pl.ds(owner * share, share), :]

    def spread(j, owner, slot, src, to_right, to_left):
        dst = block(j, owner)
        out = [(None, send(src, dst, s_sib.at[j, slot], recv.at[j, owner], sib))]
        if to_right:
            out.append((chip < chips - 1,
                        send(src, dst, s_right.at[j, slot], recv.at[j, owner], line(1))))
        if to_left:
            out.append((chip > 0,
                        send(src, dst, s_left.at[j, slot], recv.at[j, owner], line(-1))))
        return out

    def start(copies):
        for cond, copy in copies[::-1]:
            if cond is None:
                copy.start()
            else:
                pl.when(cond)(copy.start)

    def finish(copies):
        for cond, copy in copies:
            if cond is None:
                copy.wait_send()
            else:
                pl.when(cond)(copy.wait_send)

    mine = {2: spread(2, row, 0, go, True, True)}
    start(mine[2])
    a, b = xa[...].astype(F32), xb[...].astype(F32)
    moments = []
    for v in (a, b):
        moments += [jnp.sum(v, 1, keepdims=True), jnp.sum(v * v, 1, keepdims=True)]
    st_own[...] = lanes_of(moments)
    st_copies = [send(st_own, st_in.at[i], st_send.at[i], st_recv.at[i], p)
                 for i, p in enumerate(cols)]
    for copy in st_copies:
        copy.start()
    block(2, row)[...] = go[...]
    for copy in st_copies:
        copy.wait()
    total = st_own[...]
    for i in range(C - 1):
        total = total + st_in[i]
    stats[...] = total
    for j, x, at in ((1, xb, 2), (0, xa, 0)):
        hat, _ = normal_of(x[...].astype(F32), total, at, width)
        block(j, row)[...] = (hat * gain[...]).astype(BF16)
        mine[j] = spread(j, row, 0, block(j, row), True, True)
        start(mine[j])

    def relays(j, visit):
        for step in range(1, chips):
            for sign in (-1, 1):
                ok = chip >= step if sign < 0 else chip + step < chips

                @pl.when(ok)
                def _():
                    owner = row + 2 * sign * step
                    slot = step if sign < 0 else chips - 1 + step
                    visit(owner, sign, spread(j, owner, slot, block(j, owner), sign < 0, sign > 0))

    def gathered(j):
        def visit(owner, sign, copies):
            arrived(block(j, owner), recv.at[j, owner], line(sign))
            start(copies)

        relays(j, visit)
        for chip_of in range(chips):
            owner = 2 * chip_of + 1 - core
            arrived(block(j, owner), recv.at[j, owner], sib)

    def multiply(j, q, put):
        @pl.loop(0, wide // tile)
        def _(t):
            at = pl.ds(pl.multiple_of(t * tile, tile), tile)
            left = full[j, pl.ds(q * tokens, tokens), :]
            if j == 2:
                piece = lax.dot_general(left, w_down[at, :], (((1,), (1,)), ((), ())),
                                        preferred_element_type=F32)
            else:
                piece = jnp.dot(left, w_up[:, at], preferred_element_type=F32)
            put(t, piece)

    def into(j, base):
        def put(t, piece):
            buf[j, base + t // 2, :, pl.ds(pl.multiple_of((t % 2) * tile, tile), tile)] = piece
        return put

    def keep(j):
        def put(t, piece):
            own[j, t // 2, :, pl.ds(pl.multiple_of((t % 2) * tile, tile), tile)] = piece
        return put

    target = (peer_x, peer_y, peer_x, peer_x, peer_y, peer_y)

    def hop(j, s):
        return send(buf.at[j, s], inb.at[j, s], sem_s.at[j, s], sem_r.at[j, s], target[s])

    def products(j):
        multiply(j, diag, into(j, 0))
        hop(j, 0).start()
        hop(j, 1).start()
        multiply(j, flip_x, into(j, 2))
        hop(j, 2).start()
        multiply(j, flip_y, into(j, 4))
        hop(j, 5).start()
        multiply(j, col, keep(j))

    def transit(j):
        hop(j, 0).wait_recv()
        buf[j, 4] = buf[j, 4] + inb[j, 0]
        hop(j, 4).start()
        hop(j, 1).wait_recv()
        buf[j, 3] = buf[j, 3] + inb[j, 1]
        hop(j, 3).start()

    def landed(j):
        for s in range(2, 6):
            hop(j, s).wait_recv()

    def summed(j, h, at):
        return own[j, h, at, :] + inb[j, 2 + h, at, :] + inb[j, 4 + h, at, :]

    chunk = 16

    def over(body):
        @pl.loop(0, tokens // chunk)
        def _(i):
            for h in range(2):
                body(h, pl.ds(pl.multiple_of(i * chunk, chunk), chunk))

    def first(k, which):
        peer = (peer_x, peer_y)[which]
        return send(out_send.at[k], acts.at[k, pl.ds(col * tokens, tokens), :], g_s.at[k, which], g_r.at[k, which], peer)

    def relay(k, which):
        owner = (flip_x, flip_y)[which]
        ref = acts.at[k, pl.ds(owner * tokens, tokens), pl.ds(which * half, half)]
        return send(ref, ref, g_s.at[k, 2 + which], g_r.at[k, 2 + which], (peer_y, peer_x)[which])

    def publish(k):
        first(k, 0).start()
        first(k, 1).start()

    def pass_on(k):
        first(k, 0).wait_recv()
        relay(k, 0).start()
        first(k, 1).wait_recv()
        relay(k, 1).start()

    def backward(h, at):
        v = summed(1, h, at)
        phi = 0.5 * (1.0 + lax.erf(v * 0.7071067811865476))
        g = summed(2, h, at)
        slope = phi + v * jnp.exp(-0.5 * v * v) * 0.3989422804014327
        out_send[1, at, h * half : (h + 1) * half] = (v * phi).astype(BF16)
        out_send[2, at, h * half : (h + 1) * half] = (g * slope).astype(BF16)

    def forward(h, at):
        v = summed(0, h, at)
        out_send[0, at, h * half : (h + 1) * half] = (
            0.5 * v * (1.0 + lax.erf(v * 0.7071067811865476))).astype(BF16)

    rows, broad = sums.shape[1], sums.shape[2]
    step_n = broad // 4
    order = []
    low, high = 0, chips - 1
    while low <= high:
        order.append(high)
        if low < high:
            order.append(low)
        low, high = low + 1, high - 1

    def to_sib(j, z):
        return send(part.at[j, z, 1 - core], from_sib.at[j, z], sib_s.at[j, z], sib_r.at[j, z], sib)

    def to_right(j, z):
        return send(part.at[j, z, core], from_left.at[j, z], right_s.at[j, z], left_r.at[j, z], line(1))

    def to_left(j, z):
        return send(part.at[j, z, core], from_right.at[j, z], left_s.at[j, z], right_r.at[j, z], line(-1))

    def product(j, z):
        @pl.loop(0, broad // step_n)
        def _(t):
            at = pl.ds(pl.multiple_of(t * step_n, step_n), step_n)
            left = acts[2 * j, pl.ds(z * 2 * rows, 2 * rows), :]
            if j == 0:
                piece = jnp.dot(left, w_down[:, at], preferred_element_type=F32)
            else:
                piece = lax.dot_general(left, w_up[at, :], (((1,), (1,)), ((), ())),
                                        preferred_element_type=F32)
            part[j, z, 0, :, at] = piece[:rows]
            part[j, z, 1, :, at] = piece[rows:]
        to_sib(j, z).start()

    def onward(j, z):
        to_sib(j, z).wait_recv()
        part[j, z, core] = part[j, z, core] + from_sib[j, z]

        @pl.when(z > chip)
        def _():
            @pl.when(chip > 0)
            def _():
                to_right(j, z).wait_recv()
                part[j, z, core] = part[j, z, core] + from_left[j, z]

            to_right(j, z).start()

        @pl.when(z < chip)
        def _():
            @pl.when(chip < chips - 1)
            def _():
                to_left(j, z).wait_recv()
                part[j, z, core] = part[j, z, core] + from_right[j, z]

            to_left(j, z).start()


    def complete(k):
        for which in (0, 1):
            ref = acts.at[k, pl.ds(diag * tokens, tokens), pl.ds(which * half, half)]
            arrived(ref, g_r.at[k, 2 + which], (peer_y, peer_x)[which])

    gathered(2)
    load_down.wait()
    products(2)
    gathered(1)
    load_up.wait()
    products(1)
    transit(2)
    gathered(0)
    products(0)
    transit(1)
    landed(2)
    landed(1)
    transit(0)
    over(backward)
    publish(2)
    landed(0)
    over(forward)
    publish(0)
    for k in (2, 0, 1):
        acts[k, pl.ds(col * tokens, tokens), :] = out_send[k]
    pass_on(2)
    publish(1)
    complete(2)
    for z in order:
        product(1, z)
    pass_on(0)
    complete(0)
    for z in order:
        onward(1, z)
        product(0, z)
    pass_on(1)
    for z in order:
        onward(0, z)
    complete(1)
    for j in (2, 1, 0):
        finish(mine[j])
        relays(j, lambda owner, sign, copies: finish(copies))
        for which in (0, 1):
            relay(j, which).wait_send()
            first(j, which).wait_send()
        for s in range(6):
            hop(j, s).wait_send()
    for j in (0, 1):
        sums[j] = part[j, chip, core]

        @pl.when(chip > 0)
        def _():
            to_right(j, chip).wait_recv()
            sums[j] = sums[j] + from_left[j, chip]

        @pl.when(chip < chips - 1)
        def _():
            to_left(j, chip).wait_recv()
            sums[j] = sums[j] + from_right[j, chip]

    for j in (0, 1):
        for z in range(chips):
            to_sib(j, z).wait_send()
            pl.when(z > chip)(to_right(j, z).wait_send)
            pl.when(z < chip)(to_left(j, z).wait_send)


def layer(R, C, width, x_fwd, x_bwd, grad_out, gain, w_up, w_down):
    rows, columns = x_fwd.shape
    wide = w_up.shape[1]
    chips, slots = R // 2, 2 * (R // 2) - 1
    count = rows * R
    tokens, half = count // C, wide // 2
    line_block = (2, chips, rows, columns)
    return pl.pallas_call(
        functools.partial(layer_kernel, R, C, width),
        out_shape=(jax.ShapeDtypeStruct((3, count, columns), BF16),
                   jax.ShapeDtypeStruct((rows, 128), F32),
                   jax.ShapeDtypeStruct((3, count, wide), BF16),
                   jax.ShapeDtypeStruct((2, rows, columns), F32)),
        in_specs=[VMEM] * 4 + [pl.BlockSpec(memory_space=pl.ANY)] * 2,
        out_specs=(VMEM,) * 4,
        scratch_shapes=[
            pltpu.VMEM(w_up.shape, BF16), pltpu.VMEM(w_down.shape, BF16),
            pltpu.VMEM((rows, 128), F32), pltpu.VMEM((C - 1, rows, 128), F32),
            pltpu.VMEM((3, tokens, wide), BF16),
            pltpu.VMEM((3, 6, tokens, half), F32), pltpu.VMEM((3, 6, tokens, half), F32),
            pltpu.VMEM((3, 2, tokens, half), F32),
            pltpu.VMEM((2, chips, 2, rows, columns), F32),
        ]
        + [pltpu.VMEM(line_block, F32)] * 3
        + [DMA((2,)), DMA((C - 1,)), DMA((C - 1,)),
           DMA((3, slots)), DMA((3, slots)), DMA((3, slots)), DMA((3, R)),
           DMA((3, 6)), DMA((3, 6)), DMA((3, 4)), DMA((3, 4))]
        + [DMA((2, chips))] * 6,
        compiler_params=pltpu.CompilerParams(
            collective_id=0, has_side_effects=True, vmem_limit_bytes=GRANT),
        cost_estimate=pl.CostEstimate(flops=10**10, bytes_accessed=10**7, transcendentals=0),
    )(x_fwd, x_bwd, grad_out, gain, w_up, w_down)


def final_kernel(R, C, width, gn, xb, go, gain, stats, squares, dx, g_gain, total,
                 st_own, st_in, gp_own, gp_in, tt_own, tt_in,
                 st_s, st_r, gp_s, gp_r, tt_s, tt_r):
    row, col = lax.axis_index("row"), lax.axis_index("col")
    cols = [{"row": row, "col": (col + i) % C} for i in range(1, C)]
    rows = [{"row": (row + i) % R, "col": col} for i in range(1, R)]
    greet(cols + rows)
    hat, inv = normal_of(xb[...].astype(F32), stats[...], 2, width)
    grad = gn[...]
    scaled = grad * gain[...]
    st_own[...] = lanes_of([jnp.sum(scaled, 1, keepdims=True), jnp.sum(scaled * hat, 1, keepdims=True)])
    first = [send(st_own, st_in.at[i], st_s.at[i], st_r.at[i], p) for i, p in enumerate(cols)]
    for copy in first:
        copy.start()
    wide = grad.shape[1]
    gp_own[:, :wide] = jnp.broadcast_to(jnp.sum(grad * hat, 0, keepdims=True), (8, wide))
    gp_own[:, wide:] = squares[...]
    gp_in[row] = gp_own[...]
    second = [send(gp_own, gp_in.at[row], gp_s.at[i], gp_r.at[i], p) for i, p in enumerate(rows)]
    for copy in second:
        copy.start()
    for copy in second:
        copy.wait()
    gains = gp_in[0]
    for i in range(1, R):
        gains = gains + gp_in[i]
    gained = gains[:, :wide]
    g_gain[...] = gained
    tt_own[...] = gains[:, wide:] + jnp.sum(gained * gained, 1, keepdims=True)
    tt_in[col] = tt_own[...]
    third = [send(tt_own, tt_in.at[col], tt_s.at[i], tt_r.at[i], p) for i, p in enumerate(cols)]
    for copy in third:
        copy.start()
    for copy in first:
        copy.wait()
    sums = st_own[...]
    for i in range(C - 1):
        sums = sums + st_in[i]
    c1, c2 = sums[:, 0:1] / width, sums[:, 1:2] / width
    dx[...] = (go[...].astype(F32) + inv * (scaled - c1 - hat * c2)).astype(BF16)
    for copy in third:
        copy.wait()
    whole = tt_in[0]
    for i in range(1, C):
        whole = whole + tt_in[i]
    total[...] = whole


def final(R, C, width, gn, x_bwd, grad_out, gain, stats, squares):
    rows, wide = gn.shape
    return pl.pallas_call(
        functools.partial(final_kernel, R, C, width),
        out_shape=(jax.ShapeDtypeStruct((rows, wide), BF16),
                   jax.ShapeDtypeStruct((8, wide), F32),
                   jax.ShapeDtypeStruct((8, 128), F32)),
        in_specs=[VMEM] * 6,
        out_specs=(VMEM, VMEM, VMEM),
        scratch_shapes=[
            pltpu.VMEM((rows, 128), F32), pltpu.VMEM((C - 1, rows, 128), F32),
            pltpu.VMEM((8, wide + 128), F32), pltpu.VMEM((R, 8, wide + 128), F32),
            pltpu.VMEM((8, 128), F32), pltpu.VMEM((C, 8, 128), F32),
            DMA((C - 1,)), DMA((C - 1,)), DMA((R - 1,)), DMA((R - 1,)), DMA((C - 1,)), DMA((C - 1,)),
        ],
        compiler_params=pltpu.CompilerParams(
            collective_id=3, has_side_effects=True, vmem_limit_bytes=GRANT),
        cost_estimate=pl.CostEstimate(flops=10**9, bytes_accessed=10**7, transcendentals=0),
    )(gn, x_bwd, grad_out, gain, stats, squares)


def with_kernels(R, C):
    def step(x_fwd, x_bwd, grad_out, gain, w_up, w_down):
        rows, columns = x_fwd.shape
        width = columns * C
        gain_row = gain.reshape(1, columns)
        full, stats, acts, sums = layer(R, C, width, x_fwd, x_bwd, grad_out, gain_row, w_up, w_down)
        y_fwd = (x_fwd.astype(F32) + sums[0]).astype(BF16)
        down_total = contract(acts[1], full[2], 0, 0)
        up_total = contract(full[1], acts[2], 0, 0)
        squares = jnp.sum(up_total * up_total) + jnp.sum(down_total * down_total)
        dx, g_gain, total = final(R, C, width, sums[1], x_bwd, grad_out, gain_row, stats,
                                  jnp.broadcast_to(squares, (8, 128)))
        param_count = 2 * width * w_up.shape[1] * R + width
        norm_value = jnp.sqrt(total[0, 0])
        grad_rms = norm_value / math.sqrt(param_count)
        factor = jnp.minimum(1.0, clip_share * math.sqrt(param_count) / norm_value)
        return (y_fwd, dx, up_total * factor, down_total * factor, g_gain[0] * factor, grad_rms)

    return step


def solution(mesh):
    placed = (
        P("row", "col"),
        P("row", "col"),
        P("row", "col"),
        P("col"),
        P("col", "row"),
        P("row", "col"),
    )
    R, C = mesh.shape["row"], mesh.shape["col"]
    body = with_kernels(R, C) if C == 4 and R % 2 == 0 else on_device
    return jax.shard_map(
        body,
        mesh=mesh,
        in_specs=placed,
        out_specs=(
            P("row", "col"),
            P("row", "col"),
            P("col", "row"),
            P("row", "col"),
            P("col"),
            P(),
        ),
        check_vma=False,
    )
```

profile of v0, /device:TPU:0, one launch (start us, length us, event | category | flops | bytes accessed | tf_op | source)
XLA Modules:
  0.0 275.3 jit_solution(7247534866105118429)
XLA Ops:
  0.6 1.3 reshape.24.gain
  1.9 0.0 copy-start.1
  1.9 216.4 %shard_map.109 = (bf16[3,512,1536]{2,1,0:T(8,128)(2,1)}, f32[64,128]{1,0:T(8,128)}, bf16[3,512,1536]{2,1,0:T(8,128)(2,1)}, f32[2,64,1536]{2,1,0:T(8,128)}) custom-call(bf16[64,1536]{1,0:T(8,128)(2,1)} %xa.1, bf16[64,1536]{1,0:T(8,128)(2,1)} %xb.3, bf16[64,1536]{1,0:T(8,128)(2,1)} %go.3, f32[1,1536]{1,0:T(1,128)} %reshape.24.gain, ...), custom_call_target="tpu_custom_call" | custom-call | flops 10000000000 | bytes 10000000 | tf_op jit(solution)/shard_map/pallas_call | solution.py:505
  218.3 0.0 copy-done.1
  218.3 1.7 fusion.10
  220.0 1.8 slice_bitcast_fusion.gn
  221.8 8.9 %multiply_reduce_fusion = (f32[]{:T(128)}, f32[1536,1536]{1,0:T(8,128)}) fusion(bf16[3,512,1536]{2,1,0:T(8,128)(2,1)} %get-tuple-element.15, bf16[3,512,1536]{2,1,0:T(8,128)(2,1)} %get-tuple-element.16), kind=kOutput, calls=%fused_computation | convolution fusion | flops 2420637696 | bytes 12582916 | tf_op jit(solution)/shard_map/dot_general | solution.py:31
  230.7 8.9 %multiply_reduce_fusion.1 = (f32[]{:T(128)}, f32[1536,1536]{1,0:T(8,128)}) fusion(bf16[3,512,1536]{2,1,0:T(8,128)(2,1)} %get-tuple-element.16, bf16[3,512,1536]{2,1,0:T(8,128)(2,1)} %get-tuple-element.15), kind=kOutput, calls=%fused_computation.1 | convolution fusion | flops 2420637696 | bytes 12582916 | tf_op jit(solution)/shard_map/dot_general | solution.py:31
  240.8 0.6 broadcast_in_dim.3.squares
  241.4 16.0 %shard_map.110 = (bf16[64,1536]{1,0:T(8,128)(2,1)}, f32[8,1536]{1,0:T(8,128)}, f32[8,128]{1,0:T(8,128)}) custom-call(f32[64,1536]{1,0:T(8,128)} %slice_bitcast_fusion.gn, bf16[64,1536]{1,0:T(8,128)(2,1)} %xb.3, bf16[64,1536]{1,0:T(8,128)(2,1)} %go.3, f32[1,1536]{1,0:T(1,128)} %reshape.24.gain, f32[64,128]{1,0:T(8,128)} %get-tuple-element.14.stats, ...), custom_call_target="tpu_custom_call" | custom-call | flops 1000000000 | bytes 10000000 | tf_op jit(solution)/shard_map/pallas_call | solution.py:582
  257.4 1.2 slice.30
  259.4 0.0 copy-start
  259.4 12.7 %broadcast_multiply_fusion = (f32[1536,1536]{1,0:T(8,128)}, f32[1536,1536]{1,0:T(8,128)}) fusion(f32[1536,1536]{1,0:T(8,128)} %get-tuple-element.23, f32[]{:T(128)} %bitcast.6, f32[1536,1536]{1,0:T(8,128)} %get-tuple-element.21), kind=kLoop, calls=%fused_computation.2 | loop fusion | flops 4718592 | bytes 37748740 | tf_op jit(solution)/shard_map/mul | solution.py:617
  272.1 1.4 multiply_reduce_fusion.2
  273.5 0.0 copy-done
  273.5 0.7 copy.13
Async XLA Ops:
  1.9 216.4 %copy-start.1 = (bf16[64,1536]{1,0:T(8,128)(2,1)S(1)}, bf16[64,1536]{1,0:T(8,128)(2,1)}, u32[]{:S(2)}) copy-start(bf16[64,1536]{1,0:T(8,128)(2,1)} %xa.1) | copy-start | bytes 589828
  259.4 14.1 %copy-start = (bf16[64,1536]{1,0:T(8,128)(2,1)S(1)}, bf16[64,1536]{1,0:T(8,128)(2,1)}, u32[]{:S(2)}) copy-start(bf16[64,1536]{1,0:T(8,128)(2,1)} %get-tuple-element.33) | copy-start | bytes 589828
where the time goes:
time: 276 us; the launch traced here: 275 us
  Pallas kernels  232 us (84%)
  matrix products  17.7 us (6%)
  other arithmetic  15.8 us (6%)
  local copies, waits for them, and re-layouts  5.53 us (2%)
  between operations  3.83 us (1%)
    pallas_call x1, Pallas kernels, layer(): pl.pallas_call(functools.partial(layer_kernel, R, C, width), out_shape=(j...  216 us
    dot_general x2, matrix products, contract(): lax.dot_general(left, right, (((left_dim,), (right_dim,)), ((), ())), pre...  17.7 us
    pallas_call x1, Pallas kernels, final(): pl.pallas_call(functools.partial(final_kernel, R, C, width), out_shape=(j...  16 us
    mul x1, other arithmetic, step(): down_total * factor  12.7 us

commit v1 on v0

--- a/solution.py
+++ b/solution.py
@@ -146,21 +146,20 @@
     ).wait_recv()
 
 
-def greet_line(line, chip, chips, others):
-    barrier = pltpu.get_barrier_semaphore()
-    for peer in others:
-        pl.semaphore_signal(barrier, inc=1, device_id=peer, device_id_type=MESH)
-
-    @pl.when(chip > 0)
-    def _():
-        pl.semaphore_signal(barrier, inc=1, device_id=line(-1), device_id_type=MESH)
-
-    @pl.when(chip < chips - 1)
-    def _():
-        pl.semaphore_signal(barrier, inc=1, device_id=line(1), device_id_type=MESH)
-
-    beside = jnp.minimum(chip, 1) + jnp.minimum(chips - 1 - chip, 1)
-    pl.semaphore_wait(barrier, len(others) + beside)
+SPAN = 252.0
+
+
+def encode(values):
+    size = jnp.abs(values)
+    peak = jnp.maximum(jnp.max(size, 0, keepdims=True), 1e-30)
+    code = jnp.exp2(size * (SPAN / peak) - 0.5 * SPAN)
+    return jnp.where(values < 0.0, -code, code).astype(BF16), peak
+
+
+def decode(codes, peak):
+    code = codes.astype(F32)
+    size = jnp.log(jnp.abs(code)) * (peak * (1.4426950408889634 / SPAN)) + 0.5 * peak
+    return jnp.where(code < 0.0, -size, size)
 
 
 def normal_of(values, stats, at, width):
@@ -180,10 +179,10 @@
 
 
 def layer_kernel(R, C, width, xa, xb, go, gain, w_up_hbm, w_down_hbm, full, stats, acts, sums,
-                 w_up, w_down, st_own, st_in, out_send, buf, inb, own,
-                 part, from_sib, from_left, from_right,
-                 w_sem, st_send, st_recv, s_right, s_left, s_sib, recv, sem_s, sem_r, g_s, g_r,
-                 sib_s, sib_r, right_s, left_s, left_r, right_r):
+                 w_up, w_down, st_own, st_in, out_send, buf, inb, buf_p, inb_p, hold, own,
+                 part, from_sib, zbuf, zin, zbuf_p, zin_p,
+                 w_sem, st_send, st_recv, s_right, s_left, s_sib, recv, sem_s, sem_r, pk_s, pk_r,
+                 g_s, g_r, sib_s, sib_r, z_s, z_r, zp_s, zp_r):
     row, col = lax.axis_index("row"), lax.axis_index("col")
     chips = R // 2
     chip, core = row // 2, row % 2
@@ -205,7 +204,7 @@
     load_down = pltpu.make_async_copy(w_down_hbm, w_down, w_sem.at[1])
     load_down.start()
     load_up.start()
-    greet_line(line, chip, chips, cols + [sib])
+    greet(cols + [sib] + [{"row": (row + 2 * i) % R, "col": col} for i in range(1, chips)])
 
     def block(j, owner):
         return full.at[j, pl.ds(owner * share, share), :]
@@ -280,57 +279,73 @@
             owner = 2 * chip_of + 1 - core
             arrived(block(j, owner), recv.at[j, owner], sib)
 
-    def multiply(j, q, put):
-        @pl.loop(0, wide // tile)
+    def multiply(j, q, h, put):
+        @pl.loop(0, half // tile)
         def _(t):
-            at = pl.ds(pl.multiple_of(t * tile, tile), tile)
+            at = pl.ds(pl.multiple_of(h * half + t * tile, tile), tile)
             left = full[j, pl.ds(q * tokens, tokens), :]
             if j == 2:
                 piece = lax.dot_general(left, w_down[at, :], (((1,), (1,)), ((), ())),
                                         preferred_element_type=F32)
             else:
                 piece = jnp.dot(left, w_up[:, at], preferred_element_type=F32)
-            put(t, piece)
-
-    def into(j, base):
-        def put(t, piece):
-            buf[j, base + t // 2, :, pl.ds(pl.multiple_of((t % 2) * tile, tile), tile)] = piece
+            put(pl.ds(pl.multiple_of(t * tile, tile), tile), piece)
+
+    def into(j, s):
+        def put(at, piece):
+            buf[j, s, :, at], buf_p[j, s, :, at] = encode(piece)
         return put
 
-    def keep(j):
-        def put(t, piece):
-            own[j, t // 2, :, pl.ds(pl.multiple_of((t % 2) * tile, tile), tile)] = piece
+    def keep(ref, j, h):
+        def put(at, piece):
+            ref[j, h, :, at] = piece
         return put
 
     target = (peer_x, peer_y, peer_x, peer_x, peer_y, peer_y)
 
     def hop(j, s):
-        return send(buf.at[j, s], inb.at[j, s], sem_s.at[j, s], sem_r.at[j, s], target[s])
+        return (send(buf.at[j, s], inb.at[j, s], sem_s.at[j, s], sem_r.at[j, s], target[s]),
+                send(buf_p.at[j, s], inb_p.at[j, s], pk_s.at[j, s], pk_r.at[j, s], target[s]))
+
+    def go_hop(j, s):
+        for copy in hop(j, s):
+            copy.start()
+
+    def got_hop(j, s):
+        for copy in hop(j, s):
+            copy.wait_recv()
 
     def products(j):
-        multiply(j, diag, into(j, 0))
-        hop(j, 0).start()
-        hop(j, 1).start()
-        multiply(j, flip_x, into(j, 2))
-        hop(j, 2).start()
-        multiply(j, flip_y, into(j, 4))
-        hop(j, 5).start()
-        multiply(j, col, keep(j))
+        multiply(j, diag, 0, into(j, 0))
+        go_hop(j, 0)
+        multiply(j, diag, 1, into(j, 1))
+        go_hop(j, 1)
+        multiply(j, flip_x, 0, into(j, 2))
+        go_hop(j, 2)
+        multiply(j, flip_y, 1, into(j, 5))
+        go_hop(j, 5)
+        multiply(j, flip_y, 0, keep(hold, j, 0))
+        multiply(j, flip_x, 1, keep(hold, j, 1))
+        multiply(j, col, 0, keep(own, j, 0))
+        multiply(j, col, 1, keep(own, j, 1))
 
     def transit(j):
-        hop(j, 0).wait_recv()
-        buf[j, 4] = buf[j, 4] + inb[j, 0]
-        hop(j, 4).start()
-        hop(j, 1).wait_recv()
-        buf[j, 3] = buf[j, 3] + inb[j, 1]
-        hop(j, 3).start()
+        for s, onward_s in ((0, 4), (1, 3)):
+            got_hop(j, s)
+            @pl.loop(0, half // tile)
+            def _(t):
+                at = pl.ds(pl.multiple_of(t * tile, tile), tile)
+                merged = hold[j, s, :, at] + decode(inb[j, s, :, at], inb_p[j, s, :, at])
+                buf[j, onward_s, :, at], buf_p[j, onward_s, :, at] = encode(merged)
+            go_hop(j, onward_s)
 
     def landed(j):
         for s in range(2, 6):
-            hop(j, s).wait_recv()
+            got_hop(j, s)
 
     def summed(j, h, at):
-        return own[j, h, at, :] + inb[j, 2 + h, at, :] + inb[j, 4 + h, at, :]
+        return (own[j, h, at, :] + decode(inb[j, 2 + h, at, :], inb_p[j, 2 + h])
+                + decode(inb[j, 4 + h, at, :], inb_p[j, 4 + h]))
 
     chunk = 16
 
@@ -385,11 +400,10 @@
     def to_sib(j, z):
         return send(part.at[j, z, 1 - core], from_sib.at[j, z], sib_s.at[j, z], sib_r.at[j, z], sib)
 
-    def to_right(j, z):
-        return send(part.at[j, z, core], from_left.at[j, z], right_s.at[j, z], left_r.at[j, z], line(1))
-
-    def to_left(j, z):
-        return send(part.at[j, z, core], from_right.at[j, z], left_s.at[j, z], right_r.at[j, z], line(-1))
+    def to_owner(j, z):
+        peer = {"row": 2 * z + core, "col": col}
+        return (send(zbuf.at[j, z], zin.at[j, chip], z_s.at[j, z], z_r.at[j, chip], peer),
+                send(zbuf_p.at[j, z], zin_p.at[j, chip], zp_s.at[j, z], zp_r.at[j, chip], peer))
 
     def product(j, z):
         @pl.loop(0, broad // step_n)
@@ -407,26 +421,16 @@
 
     def onward(j, z):
         to_sib(j, z).wait_recv()
-        part[j, z, core] = part[j, z, core] + from_sib[j, z]
-
-        @pl.when(z > chip)
+
+        @pl.when(z != chip)
         def _():
-            @pl.when(chip > 0)
-            def _():
-                to_right(j, z).wait_recv()
-                part[j, z, core] = part[j, z, core] + from_left[j, z]
-
-            to_right(j, z).start()
-
-        @pl.when(z < chip)
-        def _():
-            @pl.when(chip < chips - 1)
-            def _():
-                to_left(j, z).wait_recv()
-                part[j, z, core] = part[j, z, core] + from_right[j, z]
-
-            to_left(j, z).start()
-
+            @pl.loop(0, broad // step_n)
+            def _(t):
+                at = pl.ds(pl.multiple_of(t * step_n, step_n), step_n)
+                zbuf[j, z, :, at], zbuf_p[j, z, :, at] = encode(
+                    part[j, z, core, :, at] + from_sib[j, z, :, at])
+            for copy in to_owner(j, z):
+                copy.start()
 
     def complete(k):
         for which in (0, 1):
@@ -474,25 +478,26 @@
             relay(j, which).wait_send()
             first(j, which).wait_send()
         for s in range(6):
-            hop(j, s).wait_send()
+            for copy in hop(j, s):
+                copy.wait_send()
     for j in (0, 1):
-        sums[j] = part[j, chip, core]
-
-        @pl.when(chip > 0)
-        def _():
-            to_right(j, chip).wait_recv()
-            sums[j] = sums[j] + from_left[j, chip]
-
-        @pl.when(chip < chips - 1)
-        def _():
-            to_left(j, chip).wait_recv()
-            sums[j] = sums[j] + from_right[j, chip]
+        sums[j] = part[j, chip, core] + from_sib[j, chip]
+        for z in range(chips):
+            @pl.when(z != chip)
+            def _():
+                peer = {"row": 2 * z + core, "col": col}
+                arrived(zin.at[j, z], z_r.at[j, z], peer)
+                arrived(zin_p.at[j, z], zp_r.at[j, z], peer)
+                sums[j] = sums[j] + decode(zin[j, z], zin_p[j, z])
 
     for j in (0, 1):
         for z in range(chips):
             to_sib(j, z).wait_send()
-            pl.when(z > chip)(to_right(j, z).wait_send)
-            pl.when(z < chip)(to_left(j, z).wait_send)
+
+            @pl.when(z != chip)
+            def _():
+                for copy in to_owner(j, z):
+                    copy.wait_send()
 
 
 def layer(R, C, width, x_fwd, x_bwd, grad_out, gain, w_up, w_down):
@@ -501,7 +506,6 @@
     chips, slots = R // 2, 2 * (R // 2) - 1
     count = rows * R
     tokens, half = count // C, wide // 2
-    line_block = (2, chips, rows, columns)
     return pl.pallas_call(
         functools.partial(layer_kernel, R, C, width),
         out_shape=(jax.ShapeDtypeStruct((3, count, columns), BF16),
@@ -514,14 +518,17 @@
             pltpu.VMEM(w_up.shape, BF16), pltpu.VMEM(w_down.shape, BF16),
             pltpu.VMEM((rows, 128), F32), pltpu.VMEM((C - 1, rows, 128), F32),
             pltpu.VMEM((3, tokens, wide), BF16),
-            pltpu.VMEM((3, 6, tokens, half), F32), pltpu.VMEM((3, 6, tokens, half), F32),
-            pltpu.VMEM((3, 2, tokens, half), F32),
+            pltpu.VMEM((3, 6, tokens, half), BF16), pltpu.VMEM((3, 6, tokens, half), BF16),
+            pltpu.VMEM((3, 6, 1, half), F32), pltpu.VMEM((3, 6, 1, half), F32),
+            pltpu.VMEM((3, 2, tokens, half), F32), pltpu.VMEM((3, 2, tokens, half), F32),
             pltpu.VMEM((2, chips, 2, rows, columns), F32),
+            pltpu.VMEM((2, chips, rows, columns), F32),
+            pltpu.VMEM((2, chips, rows, columns), BF16), pltpu.VMEM((2, chips, rows, columns), BF16),
+            pltpu.VMEM((2, chips, 1, columns), F32), pltpu.VMEM((2, chips, 1, columns), F32),
         ]
-        + [pltpu.VMEM(line_block, F32)] * 3
         + [DMA((2,)), DMA((C - 1,)), DMA((C - 1,)),
            DMA((3, slots)), DMA((3, slots)), DMA((3, slots)), DMA((3, R)),
-           DMA((3, 6)), DMA((3, 6)), DMA((3, 4)), DMA((3, 4))]
+           DMA((3, 6)), DMA((3, 6)), DMA((3, 6)), DMA((3, 6)), DMA((3, 4)), DMA((3, 4))]
         + [DMA((2, chips))] * 6,
         compiler_params=pltpu.CompilerParams(
             collective_id=0, has_side_effects=True, vmem_limit_bytes=GRANT),

time: 276 us -> 216 us (0.78)
  Pallas kernels: 232 us -> 172 us
    pallas_call x1, Pallas kernels: 216 us -> 150 us  [layer(): pl.pallas_call(functools.partial(layer_kernel, R, C, width), out_shape=(j...]
    pallas_call x1, Pallas kernels: 16 us -> 22.3 us  [final(): pl.pallas_call(functools.partial(final_kernel, R, C, width), out_shape=(j...]
where the time goes in v1:
time: 216 us; the launch traced here: 215 us
  Pallas kernels  172 us (80%)
  matrix products  17.7 us (8%)
  other arithmetic  15.8 us (7%)
  local copies, waits for them, and re-layouts  5.53 us (3%)
  between operations  3.83 us (2%)
    pallas_call x1, Pallas kernels, layer(): pl.pallas_call(functools.partial(layer_kernel, R, C, width), out_shape=(j...  150 us
    pallas_call x1, Pallas kernels, final(): pl.pallas_call(functools.partial(final_kernel, R, C, width), out_shape=(j...  22.3 us
    dot_general x2, matrix products, contract(): lax.dot_general(left, right, (((left_dim,), (right_dim,)), ((), ())), pre...  17.7 us
    mul x1, other arithmetic, step(): down_total * factor  12.7 us

profile of v1, /device:TPU:0, one launch (start us, length us, event | category | flops | bytes accessed | tf_op | source)
XLA Modules:
  0.0 215.2 jit_solution(2592100580338927831)
XLA Ops:
  0.6 1.3 reshape.24.gain
  1.9 0.0 copy-start.1
  1.9 150.0 %shard_map.109 = (bf16[3,512,1536]{2,1,0:T(8,128)(2,1)}, f32[64,128]{1,0:T(8,128)}, bf16[3,512,1536]{2,1,0:T(8,128)(2,1)}, f32[2,64,1536]{2,1,0:T(8,128)}) custom-call(bf16[64,1536]{1,0:T(8,128)(2,1)} %xa.1, bf16[64,1536]{1,0:T(8,128)(2,1)} %xb.3, bf16[64,1536]{1,0:T(8,128)(2,1)} %go.3, f32[1,1536]{1,0:T(1,128)} %reshape.24.gain, ...), custom_call_target="tpu_custom_call" | custom-call | flops 10000000000 | bytes 10000000 | tf_op jit(solution)/shard_map/pallas_call | solution.py:509
  151.9 0.0 copy-done.1
  151.9 1.7 fusion.10
  153.6 1.8 slice_bitcast_fusion.gn
  155.4 8.9 %multiply_reduce_fusion = (f32[]{:T(128)}, f32[1536,1536]{1,0:T(8,128)}) fusion(bf16[3,512,1536]{2,1,0:T(8,128)(2,1)} %get-tuple-element.15, bf16[3,512,1536]{2,1,0:T(8,128)(2,1)} %get-tuple-element.16), kind=kOutput, calls=%fused_computation | convolution fusion | flops 2420637696 | bytes 12582916 | tf_op jit(solution)/shard_map/dot_general | solution.py:31
  164.2 8.9 %multiply_reduce_fusion.1 = (f32[]{:T(128)}, f32[1536,1536]{1,0:T(8,128)}) fusion(bf16[3,512,1536]{2,1,0:T(8,128)(2,1)} %get-tuple-element.16, bf16[3,512,1536]{2,1,0:T(8,128)(2,1)} %get-tuple-element.15), kind=kOutput, calls=%fused_computation.1 | convolution fusion | flops 2420637696 | bytes 12582916 | tf_op jit(solution)/shard_map/dot_general | solution.py:31
  174.4 0.6 broadcast_in_dim.3.squares
  175.0 22.3 %shard_map.110 = (bf16[64,1536]{1,0:T(8,128)(2,1)}, f32[8,1536]{1,0:T(8,128)}, f32[8,128]{1,0:T(8,128)}) custom-call(f32[64,1536]{1,0:T(8,128)} %slice_bitcast_fusion.gn, bf16[64,1536]{1,0:T(8,128)(2,1)} %xb.3, bf16[64,1536]{1,0:T(8,128)(2,1)} %go.3, f32[1,1536]{1,0:T(1,128)} %reshape.24.gain, f32[64,128]{1,0:T(8,128)} %get-tuple-element.14.stats, ...), custom_call_target="tpu_custom_call" | custom-call | flops 1000000000 | bytes 10000000 | tf_op jit(solution)/shard_map/pallas_call | solution.py:589
  197.3 1.2 slice.30
  199.3 0.0 copy-start
  199.3 12.7 %broadcast_multiply_fusion = (f32[1536,1536]{1,0:T(8,128)}, f32[1536,1536]{1,0:T(8,128)}) fusion(f32[1536,1536]{1,0:T(8,128)} %get-tuple-element.23, f32[]{:T(128)} %bitcast.6, f32[1536,1536]{1,0:T(8,128)} %get-tuple-element.21), kind=kLoop, calls=%fused_computation.2 | loop fusion | flops 4718592 | bytes 37748740 | tf_op jit(solution)/shard_map/mul | solution.py:624
  212.0 1.4 multiply_reduce_fusion.2
  213.4 0.0 copy-done
  213.4 0.7 copy.13
Async XLA Ops:
  1.9 150.0 %copy-start.1 = (bf16[64,1536]{1,0:T(8,128)(2,1)S(1)}, bf16[64,1536]{1,0:T(8,128)(2,1)}, u32[]{:S(2)}) copy-start(bf16[64,1536]{1,0:T(8,128)(2,1)} %xa.1) | copy-start | bytes 589828
  199.3 14.1 %copy-start = (bf16[64,1536]{1,0:T(8,128)(2,1)S(1)}, bf16[64,1536]{1,0:T(8,128)(2,1)}, u32[]{:S(2)}) copy-start(bf16[64,1536]{1,0:T(8,128)(2,1)} %get-tuple-element.33) | copy-start | bytes 589828

commit v2 on v1

v2 whole, which is shorter than its diff:
```python
import functools
import math

import jax
import jax.numpy as jnp
from jax import lax
from jax.experimental import pallas as pl
from jax.experimental.pallas import tpu as pltpu
from jax.sharding import PartitionSpec as P

D = 6144
FF = 12288


eps = 1e-06
clip_share = 0.25


def erf_gelu(value):
    return 0.5 * value * (1.0 + lax.erf(value * 0.7071067811865476))


def gelu_slope(value):
    return (
        0.5 * (1.0 + lax.erf(value * 0.7071067811865476))
        + value * jnp.exp(-0.5 * value * value) * 0.3989422804014327
    )


def contract(left, right, left_dim, right_dim):
    return lax.dot_general(
        left, right, (((left_dim,), (right_dim,)), ((), ())), preferred_element_type=jnp.float32
    )


def row_sums(tokens):
    values = tokens.astype(jnp.float32)
    return (jnp.sum(values, -1), jnp.sum(values * values, -1))


def normalize(tokens, first, second):
    values = tokens.astype(jnp.float32)
    centre = first / D
    spread = second / D - centre * centre
    inv_scale = lax.rsqrt(spread + eps)
    return ((values - centre[:, None]) * inv_scale[:, None], inv_scale)


def up_both(normed_a, normed_b, w_up):
    full_a, full_b = (
        lax.all_gather(normed_a, "row", axis=0, tiled=True),
        lax.all_gather(normed_b, "row", axis=0, tiled=True),
    )
    width = w_up.shape[1]
    summed = lax.psum_scatter(
        jnp.concatenate(
            [
                jnp.dot(full_a, w_up, preferred_element_type=jnp.float32),
                jnp.dot(full_b, w_up, preferred_element_type=jnp.float32),
            ],
            1,
        ),
        "col",
        scatter_dimension=0,
        tiled=True,
    )
    return (summed[:, :width], summed[:, width:], full_b)


def on_device(x_fwd, x_bwd, grad_out, gain, w_up, w_down):
    first_a, second_a = row_sums(x_fwd)
    first_b, second_b = row_sums(x_bwd)
    first_a, second_a, first_b, second_b = lax.psum((first_a, second_a, first_b, second_b), "col")
    centred_a, _ = normalize(x_fwd, first_a, second_a)
    centred_b, inv_scale = normalize(x_bwd, first_b, second_b)
    normed_a = (centred_a * gain).astype(jnp.bfloat16)
    normed_b = (centred_b * gain).astype(jnp.bfloat16)
    pre_a, pre_b, normed_full = up_both(normed_a, normed_b, w_up)
    hidden_a = erf_gelu(pre_a).astype(jnp.bfloat16)
    output_part = jnp.dot(
        lax.all_gather(hidden_a, "col", axis=0, tiled=True),
        w_down,
        preferred_element_type=jnp.float32,
    )
    output_sum = lax.psum_scatter(output_part, "row", scatter_dimension=0, tiled=True)
    y_fwd = (x_fwd.astype(jnp.float32) + output_sum).astype(jnp.bfloat16)
    hidden_b = erf_gelu(pre_b).astype(jnp.bfloat16)
    grad_full = lax.all_gather(grad_out, "row", axis=0, tiled=True)
    grad_hidden = lax.psum_scatter(
        contract(grad_full, w_down, 1, 1), "col", scatter_dimension=0, tiled=True
    )
    grad_pre = (grad_hidden * gelu_slope(pre_b)).astype(jnp.bfloat16)
    hidden_piece = lax.all_gather(hidden_b, "col", axis=0, tiled=True)
    pre_piece = lax.all_gather(grad_pre, "col", axis=0, tiled=True)
    down_total = contract(hidden_piece, grad_full, 0, 0)
    up_total = contract(normed_full, pre_piece, 0, 0)
    input_total = contract(pre_piece, w_up, 1, 1)
    grad_normed = lax.psum_scatter(input_total, "row", scatter_dimension=0, tiled=True)
    scaled = grad_normed * gain
    first_back = jnp.sum(scaled, -1)
    second_back = jnp.sum(scaled * centred_b, -1)
    first_back, second_back = lax.psum((first_back, second_back), "col")
    dx_bwd = (
        grad_out.astype(jnp.float32)
        + inv_scale[:, None]
        * (scaled - first_back[:, None] / D - centred_b * (second_back[:, None] / D))
    ).astype(jnp.bfloat16)
    gain_part = jnp.sum(grad_normed * centred_b, 0)
    weight_squares = jnp.sum(up_total * up_total) + jnp.sum(down_total * down_total)
    g_gain = lax.psum(gain_part, "row")
    first_row = (lax.axis_index("row") == 0).astype(jnp.float32)
    total = lax.psum(weight_squares + first_row * jnp.sum(g_gain * g_gain), ("row", "col"))
    param_count = 2 * D * FF + D
    norm_value = jnp.sqrt(total)
    grad_rms = norm_value / math.sqrt(param_count)
    factor = jnp.minimum(1.0, clip_share * math.sqrt(param_count) / norm_value)
    return (y_fwd, dx_bwd, up_total * factor, down_total * factor, g_gain * factor, grad_rms)


MESH = pl.DeviceIdType.MESH
VMEM = pl.BlockSpec(memory_space=pltpu.VMEM)
F32 = jnp.float32
BF16 = jnp.bfloat16
DMA = pltpu.SemaphoreType.DMA
GRANT = 45 * 1024 * 1024


def send(src, dst, send_sem, recv_sem, peer):
    return pltpu.make_async_remote_copy(
        src_ref=src, dst_ref=dst, send_sem=send_sem, recv_sem=recv_sem,
        device_id=peer, device_id_type=MESH,
    )


def arrived(ref, sem, peer):
    pltpu.make_async_remote_copy(
        src_ref=ref, dst_ref=ref, send_sem=sem, recv_sem=sem,
        device_id=peer, device_id_type=MESH,
    ).wait_recv()


SPAN = 252.0


def encode(values):
    size = jnp.abs(values)
    peak = jnp.maximum(jnp.max(size, 0, keepdims=True), 1e-30)
    code = jnp.exp2(size * (SPAN / peak) - 0.5 * SPAN)
    return jnp.where(values < 0.0, -code, code).astype(BF16), peak


def decode(codes, peak):
    code = codes.astype(F32)
    size = jnp.log(jnp.abs(code)) * (peak * (1.4426950408889634 / SPAN)) + 0.5 * peak
    return jnp.where(code < 0.0, -size, size)


def normal_of(values, stats, at, width):
    centre = stats[:, at : at + 1] / width
    spread = stats[:, at + 1 : at + 2] / width - centre * centre
    inv = lax.rsqrt(spread + eps)
    return (values - centre) * inv, inv


def lanes_of(columns):
    rows = columns[0].shape[0]
    lane = lax.broadcasted_iota(jnp.int32, (rows, 128), 1)
    out = jnp.zeros((rows, 128), F32)
    for i, column in enumerate(columns):
        out = jnp.where(lane == i, column, out)
    return out


def step_kernel(R, C, width, params, xa, xb, go, gain, w_up_hbm, w_down_hbm,
                g_up, g_down, y, dx, gained, verdict,
                full, acts, w_up, w_down, gain_row, st_own, st_in, keep, buf, inb, buf_p, inb_p,
                part, from_sib, zbuf, zin, zbuf_p, zin_p, mine, sq,
                back_own, back_in, gp_own, gp_in, tt_own, tt_in, uu_own, uu_in,
                w_sem, st_s, st_r, s_right, s_left, s_sib, recv, hop_s, hop_r, peak_s, peak_r,
                g_s, g_r, sib_s, sib_r, z_s, z_r, zp_s, zp_r,
                back_s, back_r, gp_s, gp_r, tt_s, tt_r, uu_s, uu_r):
    row, col = lax.axis_index("row"), lax.axis_index("col")
    chips = R // 2
    chip, core = row // 2, row % 2
    sib = {"row": row + 1 - 2 * core, "col": col}
    cols = [{"row": row, "col": (col + i) % C} for i in range(1, C)]
    rows_of = [{"row": (row + i) % R, "col": col} for i in range(1, R)]
    flip_x = col + 1 - 2 * (col % 2)
    flip_y = (col + 2) % 4
    diag = 3 - col
    peer_x, peer_y = {"row": row, "col": flip_x}, {"row": row, "col": flip_y}
    share, columns = xa.shape
    tokens = share * R // C
    wide = w_up.shape[1]
    half = wide // 2
    tile = half // 2
    high = chip // 2

    def line(step):
        return {"row": row + 2 * step, "col": col}

    def mirror(at, on):
        return at + on * (chips - 1 - 2 * at)

    def order(k):
        low = mirror(chip, high)
        return mirror((low, 1 - low, 2, 3)[k], high)

    load_up = pltpu.make_async_copy(w_up_hbm, w_up, w_sem.at[0])
    load_down = pltpu.make_async_copy(w_down_hbm, w_down, w_sem.at[1])
    load_down.start()
    load_up.start()
    barrier = pltpu.get_barrier_semaphore()
    for peer in cols + rows_of:
        pl.semaphore_signal(barrier, inc=1, device_id=peer, device_id_type=MESH)
    moments = []
    for x in (xa, xb):
        v = x[...].astype(F32)
        moments += [jnp.sum(v, 1, keepdims=True), jnp.sum(v * v, 1, keepdims=True)]
    st_own[...] = lanes_of(moments)
    for i in range(columns // 128):
        gain_row[:, i * 128 : (i + 1) * 128] = gain[i : i + 1, :]
    sq[...] = jnp.zeros_like(sq)
    pl.semaphore_wait(barrier, len(cols) + len(rows_of))

    def block(j, owner):
        return full.at[j, pl.ds(owner * share, share), :]

    def spread(j, owner, slot, src, to_right, to_left):
        dst = block(j, owner)
        out = [(None, send(src, dst, s_sib.at[j, slot], recv.at[j, owner], sib))]
        if to_right:
            out.append((chip < chips - 1,
                        send(src, dst, s_right.at[j, slot], recv.at[j, owner], line(1))))
        if to_left:
            out.append((chip > 0,
                        send(src, dst, s_left.at[j, slot], recv.at[j, owner], line(-1))))
        return out

    def start(copies):
        for cond, copy in copies[::-1]:
            if cond is None:
                copy.start()
            else:
                pl.when(cond)(copy.start)

    def finish(copies):
        for cond, copy in copies:
            if cond is None:
                copy.wait_send()
            else:
                pl.when(cond)(copy.wait_send)

    mine_of = {2: spread(2, row, 0, go, True, True)}
    start(mine_of[2])
    st_copies = [send(st_own, st_in.at[i], st_s.at[i], st_r.at[i], p) for i, p in enumerate(cols)]
    for copy in st_copies:
        copy.start()
    block(2, row)[...] = go[...]

    def relays(j, visit, steps):
        for step in steps:
            for sign in (-1, 1):
                ok = chip >= step if sign < 0 else chip + step < chips

                @pl.when(ok)
                def _():
                    owner = row + 2 * sign * step
                    slot = step if sign < 0 else chips - 1 + step
                    visit(owner, sign, spread(j, owner, slot, block(j, owner), sign < 0, sign > 0))

    def gather(j, step):
        def visit(owner, sign, copies):
            arrived(block(j, owner), recv.at[j, owner], line(sign))
            start(copies)

        relays(j, visit, (step,))

    ends = (chip + 1) % chips < 2

    def gather_for(j, k):
        if k == 1:
            gather(j, 1)
        elif k == 2:
            pl.when(ends)(lambda: gather(j, 2))
        elif k == 3:
            pl.when(jnp.logical_not(ends))(lambda: gather(j, 2))
            pl.when(ends)(lambda: gather(j, 3))

    def hop(j, s, peer):
        return (send(buf.at[j, s], inb.at[j, s], hop_s.at[j, s], hop_r.at[j, s], peer),
                send(buf_p.at[j, s], inb_p.at[j, s], peak_s.at[j, s], peak_r.at[j, s], peer))

    def go_hop(j, s, peer):
        for copy in hop(j, s, peer):
            copy.start()

    def got_hop(j, s):
        for copy in hop(j, s, peer_x):
            copy.wait_recv()

    def over_tiles(body, size):
        @pl.loop(0, size // tile)
        def _(t):
            body(pl.ds(pl.multiple_of(t * tile, tile), tile))

    def role_of(q):
        return (q + col) % 2, (q // 2 + col // 2) % 2

    def product(j, k):
        q = order(k)
        owner = 2 * q + 1 - core
        arrived(block(j, owner), recv.at[j, owner], sib)
        off_x, off_y = role_of(q)

        @pl.loop(0, 2)
        def _(h):
            now = off_x + h * (off_y - off_x)
            slot = 2 * (1 - off_y) + h * (1 - 2 * off_x + 2 * off_y)
            s = 2 * (1 - off_y) + h * (3 - 4 * off_x + 2 * off_y)
            at = pl.ds(pl.multiple_of(h * half, half), half)
            left = full[j, pl.ds(q * tokens, tokens), :]
            if j == 2:
                piece = lax.dot_general(left, w_down[at, :], (((1,), (1,)), ((), ())),
                                        preferred_element_type=F32)
            else:
                piece = jnp.dot(left, w_up[:, at], preferred_element_type=F32)
            place = now * 12 + (1 - now) * (j * 4 + slot)
            keep[place] = piece

            @pl.when(now == 1)
            def _():
                def code(part_of):
                    buf[j, s, :, part_of], buf_p[j, s, :, part_of] = encode(keep[12, :, part_of])

                over_tiles(code, half)
                go_hop(j, s, {"row": row, "col": flip_x + h * (flip_y - flip_x)})

    def merge(j, k):
        off_x, off_y = role_of(order(k))

        @pl.when(off_x + off_y == 1)
        def _():
            got_hop(j, off_x)

            def add(at):
                merged = keep[j * 4 + off_x, :, at] + decode(inb[j, off_x, :, at], inb_p[j, off_x, :, at])
                buf[j, 4 - off_x, :, at], buf_p[j, 4 - off_x, :, at] = encode(merged)

            over_tiles(add, half)
            go_hop(j, 4 - off_x, {"row": row, "col": flip_y + off_x * (flip_x - flip_y)})

    def landed(j):
        for s in range(2, 6):
            got_hop(j, s)

    def summed(j, h, at):
        return (keep[j * 4 + 2 + h, at, :] + decode(inb[j, 2 + h, at, :], inb_p[j, 2 + h])
                + decode(inb[j, 4 + h, at, :], inb_p[j, 4 + h]))

    chunk = 16

    def over(body):
        @pl.loop(0, tokens // chunk)
        def _(i):
            at = pl.ds(pl.multiple_of(i * chunk, chunk), chunk)
            to = pl.ds(pl.multiple_of(col * tokens + i * chunk, chunk), chunk)
            for h in range(2):
                body(h, at, to, slice(h * half, (h + 1) * half))

    def backward(h, at, to, across):
        v = summed(1, h, at)
        phi = 0.5 * (1.0 + lax.erf(v * 0.7071067811865476))
        g = summed(2, h, at)
        slope = phi + v * jnp.exp(-0.5 * v * v) * 0.3989422804014327
        acts[1, to, across] = (v * phi).astype(BF16)
        acts[2, to, across] = (g * slope).astype(BF16)

    def forward(h, at, to, across):
        v = summed(0, h, at)
        acts[0, to, across] = (0.5 * v * (1.0 + lax.erf(v * 0.7071067811865476))).astype(BF16)

    def piece_of(k, owner, h):
        return acts.at[k, pl.ds(pl.multiple_of(owner * tokens, tokens), tokens), pl.ds(h * half, half)]

    def passing(k, i):
        owner, h, peer = ((col, 0, peer_x), (col, 1, peer_y), (col, 1, peer_x), (col, 0, peer_y),
                          (flip_x, 0, peer_y), (flip_y, 1, peer_x))[i]
        ref = piece_of(k, owner, h)
        return send(ref, ref, g_s.at[k, i], g_r.at[k, i], peer)

    def publish(k):
        for i in range(4):
            passing(k, i).start()

    def pass_on(k):
        arrived(piece_of(k, flip_x, 0), g_r.at[k, 0], peer_x)
        passing(k, 4).start()
        arrived(piece_of(k, flip_y, 1), g_r.at[k, 1], peer_y)
        passing(k, 5).start()

    def sides(k):
        arrived(piece_of(k, flip_x, 1), g_r.at[k, 2], peer_x)
        arrived(piece_of(k, flip_y, 0), g_r.at[k, 3], peer_y)

    def corner(k):
        arrived(piece_of(k, diag, 0), g_r.at[k, 4], peer_y)
        arrived(piece_of(k, diag, 1), g_r.at[k, 5], peer_x)

    roles = (col, flip_x, flip_y, diag)

    def to_sib(j, i):
        return send(part.at[j, i, 1 - core], from_sib.at[j, i], sib_s.at[j, i], sib_r.at[j, i], sib)

    def to_owner(j, i):
        peer = {"row": 2 * roles[i] + core, "col": col}
        return (send(zbuf.at[j, i], zin.at[j, chip], z_s.at[j, i], z_r.at[j, chip], peer),
                send(zbuf_p.at[j, i], zin_p.at[j, chip], zp_s.at[j, i], zp_r.at[j, chip], peer))

    def second(j, i):
        @pl.loop(0, 2)
        def _(h):
            at = pl.ds(pl.multiple_of(h * half, half), half)
            left = acts[2 * j, pl.ds(pl.multiple_of(roles[i] * tokens, tokens), tokens), :]
            if j == 0:
                piece = jnp.dot(left, w_down[:, at], preferred_element_type=F32)
            else:
                piece = lax.dot_general(left, w_up[at, :], (((1,), (1,)), ((), ())),
                                        preferred_element_type=F32)
            part[j, i, 0, :, at] = piece[:share]
            part[j, i, 1, :, at] = piece[share:]

        to_sib(j, i).start()

    def onward(j, i):
        to_sib(j, i).wait_recv()
        away = roles[i] != chip

        @pl.when(away)
        def _():
            def code(at):
                zbuf[j, i, :, at], zbuf_p[j, i, :, at] = encode(
                    part[j, i, core, :, at] + from_sib[j, i, :, at])

            over_tiles(code, columns)
            for copy in to_owner(j, i):
                copy.start()

        @pl.when(jnp.logical_not(away))
        def _():
            mine[j] = part[j, i, core] + from_sib[j, i]

    def collect(j):
        for z in range(chips):
            @pl.when(z != chip)
            def _():
                peer = {"row": 2 * z + core, "col": col}
                arrived(zin.at[j, z], z_r.at[j, z], peer)
                arrived(zin_p.at[j, z], zp_r.at[j, z], peer)
                mine[j] = mine[j] + decode(zin[j, z], zin_p[j, z])

    def gradient(out, left, right):
        step_m, step_n = 256, half

        @pl.loop(0, out.shape[0] // step_m)
        def _(m):
            at = pl.ds(pl.multiple_of(m * step_m, step_m), step_m)
            for n in range(out.shape[1] // step_n):
                across = slice(n * step_n, (n + 1) * step_n)
                piece = lax.dot_general(left[:, at], right[:, across], (((0,), (0,)), ((), ())),
                                        preferred_element_type=F32)
                out[at, across] = piece
                sq[:, across] = sq[:, across] + jnp.sum(piece * piece, 0, keepdims=True)

    load_down.wait()
    product(2, 0)
    gather_for(2, 1)
    for copy in st_copies:
        copy.wait()
    stats = st_own[...]
    for i in range(C - 1):
        stats = stats + st_in[i]
    for j, x, at in ((1, xb, 2), (0, xa, 0)):
        hat, _ = normal_of(x[...].astype(F32), stats, at, width)
        block(j, row)[...] = (hat * gain_row[...]).astype(BF16)
        mine_of[j] = spread(j, row, 0, block(j, row), True, True)
        if j == 1:
            start(mine_of[1])
    product(2, 1)
    merge(2, 0)
    gather_for(2, 2)
    product(2, 2)
    merge(2, 1)
    gather_for(2, 3)
    start(mine_of[0])
    load_up.wait()
    product(2, 3)
    merge(2, 2)
    product(1, 0)
    gather_for(1, 1)
    merge(2, 3)
    product(1, 1)
    merge(1, 0)
    gather_for(1, 2)
    product(1, 2)
    merge(1, 1)
    gather_for(1, 3)
    product(1, 3)
    merge(1, 2)
    product(0, 0)
    gather_for(0, 1)
    merge(1, 3)
    landed(2)
    landed(1)
    over(backward)
    publish(2)
    publish(1)
    product(0, 1)
    merge(0, 0)
    second(1, 0)
    gather_for(0, 2)
    product(0, 2)
    merge(0, 1)
    pass_on(2)
    gather_for(0, 3)
    product(0, 3)
    merge(0, 2)
    onward(1, 0)
    sides(2)
    second(1, 1)
    merge(0, 3)
    second(1, 2)
    pass_on(1)
    landed(0)
    over(forward)
    publish(0)
    onward(1, 1)
    onward(1, 2)
    corner(2)
    second(1, 3)
    second(0, 0)
    onward(1, 3)
    gradient(g_up, full.at[1], acts.at[2])
    onward(0, 0)
    sides(1)
    corner(1)
    pass_on(0)
    gradient(g_down, acts.at[1], full.at[2])
    tt_own[...] = jnp.broadcast_to(jnp.sum(sq[...], 1, keepdims=True), tt_own.shape)
    third = [send(tt_own, tt_in.at[row], tt_s.at[i], tt_r.at[i], p) for i, p in enumerate(rows_of)]
    for copy in third:
        copy.start()
    sides(0)
    second(0, 1)
    second(0, 2)
    collect(1)
    grad = mine[1]
    hat, inv = normal_of(xb[...].astype(F32), stats, 2, width)
    scaled = grad * gain_row[...]
    back_own[...] = lanes_of([jnp.sum(scaled, 1, keepdims=True), jnp.sum(scaled * hat, 1, keepdims=True)])
    first = [send(back_own, back_in.at[i], back_s.at[i], back_r.at[i], p) for i, p in enumerate(cols)]
    for copy in first:
        copy.start()
    gain_part = jnp.sum(grad * hat, 0, keepdims=True)
    for i in range(columns // 128):
        gp_own[i : i + 1, :] = gain_part[:, i * 128 : (i + 1) * 128]
    gains_out = [send(gp_own, gp_in.at[row], gp_s.at[i], gp_r.at[i], p) for i, p in enumerate(rows_of)]
    for copy in gains_out:
        copy.start()
    onward(0, 1)
    onward(0, 2)
    corner(0)
    second(0, 3)
    gp_in[row] = gp_own[...]
    tt_in[row] = tt_own[...]
    for copy in gains_out + third:
        copy.wait()
    onward(0, 3)
    gains, squares = gp_in[0], tt_in[0]
    for i in range(1, R):
        gains, squares = gains + gp_in[i], squares + tt_in[i]
    gained[...] = gains
    uu_own[...] = squares + jnp.sum(gains * gains)
    fourth = [send(uu_own, uu_in.at[col], uu_s.at[i], uu_r.at[i], p) for i, p in enumerate(cols)]
    for copy in fourth:
        copy.start()
    uu_in[col] = uu_own[...]
    for copy in first:
        copy.wait()
    sums = back_own[...]
    for i in range(C - 1):
        sums = sums + back_in[i]
    c1, c2 = sums[:, 0:1] / width, sums[:, 1:2] / width
    hat, inv = normal_of(xb[...].astype(F32), stats, 2, width)
    scaled = mine[1] * gain_row[...]
    dx[...] = (go[...].astype(F32) + inv * (scaled - c1 - hat * c2)).astype(BF16)
    for copy in fourth:
        copy.wait()
    total = uu_in[0]
    for i in range(1, C):
        total = total + uu_in[i]
    norm_value = jnp.sqrt(total)
    verdict[0] = jnp.minimum(1.0, clip_share * math.sqrt(params) / norm_value)
    verdict[1] = norm_value / math.sqrt(params)
    collect(0)
    y[...] = (xa[...].astype(F32) + mine[0]).astype(BF16)

    for j in (2, 1, 0):
        finish(mine_of[j])
        relays(j, lambda owner, sign, copies: finish(copies), range(1, chips))
        for i in range(6):
            passing(j, i).wait_send()
            for copy in hop(j, i, peer_x):
                copy.wait_send()
    for j in (0, 1):
        for i in range(chips):
            to_sib(j, i).wait_send()

            @pl.when(roles[i] != chip)
            def _():
                for copy in to_owner(j, i):
                    copy.wait_send()


def step_on_core(R, C, width, params, x_fwd, x_bwd, grad_out, gain, w_up, w_down):
    rows, columns = x_fwd.shape
    wide = w_up.shape[1]
    chips, slots = R // 2, 2 * (R // 2) - 1
    count = rows * R
    tokens, half = count // C, wide // 2
    lines = columns // 128
    VM = pltpu.VMEM
    return pl.pallas_call(
        functools.partial(step_kernel, R, C, width, params),
        out_shape=(VM((columns, wide), F32), VM((wide, columns), F32), VM((rows, columns), BF16),
                   VM((rows, columns), BF16), VM((lines, 128), F32), VM((2, 8, 128), F32)),
        in_specs=[VMEM] * 4 + [pl.BlockSpec(memory_space=pl.ANY)] * 2,
        out_specs=(VMEM,) * 6,
        scratch_shapes=[
            VM((3, count, columns), BF16), VM((3, count, wide), BF16),
            VM(w_up.shape, BF16), VM(w_down.shape, BF16), VM((1, columns), F32),
            VM((rows, 128), F32), VM((C - 1, rows, 128), F32),
            VM((13, tokens, half), F32),
            VM((3, 6, tokens, half), BF16), VM((3, 6, tokens, half), BF16),
            VM((3, 6, 1, half), F32), VM((3, 6, 1, half), F32),
            VM((2, chips, 2, rows, columns), F32), VM((2, chips, rows, columns), F32),
            VM((2, chips, rows, columns), BF16), VM((2, chips, rows, columns), BF16),
            VM((2, chips, 1, columns), F32), VM((2, chips, 1, columns), F32),
            VM((2, rows, columns), F32), VM((1, columns), F32),
            VM((rows, 128), F32), VM((C - 1, rows, 128), F32),
            VM((lines, 128), F32), VM((R, lines, 128), F32),
            VM((8, 128), F32), VM((R, 8, 128), F32), VM((8, 128), F32), VM((C, 8, 128), F32),
        ]
        + [DMA((2,)), DMA((C - 1,)), DMA((C - 1,)),
           DMA((3, slots)), DMA((3, slots)), DMA((3, slots)), DMA((3, R))]
        + [DMA((3, 6))] * 6 + [DMA((2, chips))] * 6
        + [DMA((C - 1,))] * 2 + [DMA((R - 1,))] * 4 + [DMA((C - 1,))] * 2,
        compiler_params=pltpu.CompilerParams(
            collective_id=0, has_side_effects=True, vmem_limit_bytes=GRANT),
        cost_estimate=pl.CostEstimate(flops=2 * 10**10, bytes_accessed=10**7, transcendentals=0),
    )(x_fwd, x_bwd, grad_out, gain, w_up, w_down)


def clip_kernel(g_up, g_down, y_in, dx_in, gains, verdict, up, down, y, dx, step_gain, rms, staged, sem):
    factor = verdict[0, 0:1, 0:1]
    slots = staged.shape[1]
    size = staged.shape[2]
    for which, (grad, out) in enumerate(((g_up, up), (g_down, down))):
        for i in range(slots):
            at = pl.ds(i * size, size)
            staged[which, i] = grad[at, :] * factor
            pltpu.make_async_copy(staged.at[which, i], out.at[at, :], sem.at[which, i]).start()
    y[...] = y_in[...]
    dx[...] = dx_in[...]
    step_gain[...] = gains[...] * factor
    rms[...] = verdict[1, 0:1, 0:1]
    for which, out in enumerate((up, down)):
        for i in range(slots):
            at = pl.ds(i * size, size)
            pltpu.make_async_copy(staged.at[which, i], out.at[at, :], sem.at[which, i]).wait()


def clip(g_up, g_down, y, dx, gains, verdict):
    slots = 12
    size = g_up.shape[0] // slots
    like = jax.ShapeDtypeStruct
    return pl.pallas_call(
        clip_kernel,
        out_shape=(like(g_up.shape, F32), like(g_down.shape, F32), like(y.shape, BF16),
                   like(dx.shape, BF16), like(gains.shape, F32), like((1, 1), F32)),
        in_specs=[VMEM] * 6,
        out_specs=(pl.BlockSpec(memory_space=pl.ANY),) * 2 + (VMEM,) * 4,
        scratch_shapes=[pltpu.VMEM((2, slots, size, g_up.shape[1]), F32), DMA((2, slots))],
        compiler_params=pltpu.CompilerParams(vmem_limit_bytes=40 * 1024 * 1024),
        cost_estimate=pl.CostEstimate(flops=10**8, bytes_accessed=4 * 10**7, transcendentals=0),
    )(g_up, g_down, y, dx, gains, verdict)


def with_kernels(R, C):
    def step(x_fwd, x_bwd, grad_out, gain, w_up, w_down):
        rows, columns = x_fwd.shape
        width = columns * C
        params = 2 * width * w_up.shape[1] * R + width
        parts = step_on_core(R, C, width, params, x_fwd, x_bwd, grad_out,
                             gain.reshape(columns // 128, 128), w_up, w_down)
        up, down, y, dx, step_gain, rms = clip(*parts)
        return y, dx, up, down, step_gain.reshape(columns), rms.reshape(())

    return step


def solution(mesh):
    placed = (
        P("row", "col"),
        P("row", "col"),
        P("row", "col"),
        P("col"),
        P("col", "row"),
        P("row", "col"),
    )
    R, C = mesh.shape["row"], mesh.shape["col"]
    body = with_kernels(R, C) if C == 4 and R == 8 else on_device
    return jax.shard_map(
        body,
        mesh=mesh,
        in_specs=placed,
        out_specs=(
            P("row", "col"),
            P("row", "col"),
            P("col", "row"),
            P("row", "col"),
            P("col"),
            P(),
        ),
        check_vma=False,
    )
```

time: 216 us -> 162 us (0.75)
  the two profiles are of different devices: /device:TPU:0 before, /device:TPU:24 now
where the time goes in v2:
time: 162 us
  Pallas kernels  150 us (93%)
  local copies, waits for them, and re-layouts  11 us (7%)
    pallas_call x1, Pallas kernels, step_on_core(): pl.pallas_call(functools.partial(step_kernel, R, C, width, params), out_s...  139 us
    pallas_call x1, Pallas kernels, clip(): pl.pallas_call(clip_kernel, out_shape=(like(g_up.shape, F32), like(g_down...  11.2 us
    unnamed x6, local copies, waits for them, and re-layouts  11 us

profile of v2, /device:TPU:24, one launch (start us, length us, event | category | flops | bytes accessed | tf_op | source)
XLA Modules:
  0.0 161.7 jit_solution(14407739724003431135)
XLA Ops:
  0.6 138.7 %shard_map.109 = (f32[1536,1536]{1,0:T(8,128)S(1)}, f32[1536,1536]{1,0:T(8,128)S(1)}, bf16[64,1536]{1,0:T(8,128)(2,1)S(1)}, bf16[64,1536]{1,0:T(8,128)(2,1)S(1)}...) custom-call(bf16[64,1536]{1,0:T(8,128)(2,1)} %xa.1, bf16[64,1536]{1,0:T(8,128)(2,1)} %xb.1, bf16[64,1536]{1,0:T(8,128)(2,1)} %go.1, ...), custom_call_target="tpu_custom_call" | custom-call | flops 20000000000 | bytes 10000000 | tf_op jit(solution)/shard_map/pallas_call | solution.py:633
  139.3 0.0 copy-start
  139.4 3.7 %copy-done = f32[1536,1536]{1,0:T(8,128)} copy-done((f32[1536,1536]{1,0:T(8,128)}, f32[1536,1536]{1,0:T(8,128)S(1)}, u32[]{:S(2)}) %copy-start) | copy-done | bytes 9437208
  143.1 0.0 copy-start.2
  143.1 3.6 %copy-done.2 = f32[1536,1536]{1,0:T(8,128)} copy-done((f32[1536,1536]{1,0:T(8,128)}, f32[1536,1536]{1,0:T(8,128)S(1)}, u32[]{:S(2)}) %copy-start.2) | copy-done | bytes 9437208
  146.7 0.0 copy-start.1
  146.7 3.7 %copy-done.1 = f32[1536,1536]{1,0:T(8,128)S(1)} copy-done((f32[1536,1536]{1,0:T(8,128)S(1)}, f32[1536,1536]{1,0:T(8,128)}, u32[]{:S(2)}) %copy-start.1) | copy-done | bytes 9437208
  150.4 11.2 %shard_map.110 = (f32[1536,1536]{1,0:T(8,128)}, f32[1536,1536]{1,0:T(8,128)}, bf16[64,1536]{1,0:T(8,128)(2,1)}, bf16[64,1536]{1,0:T(8,128)(2,1)}, f32[12,128]{1,0:T(8,128)}, /*index=5*/f32[1,1]{1,0:T(1,128)}) custom-call(f32[1536,1536]{1,0:T(8,128)S(1)} %copy-done.1, f32[1536,1536]{1,0:T(8,128)} %copy-done.2, bf16[64,1536]{1,0:T(8,128)(2,1)S(1)} %get-tuple-element.20.y_in, ...), custom_call_target="tpu_custom_call" | custom-call | flops 100000000 | bytes 40000000 | tf_op jit(solution)/shard_map/pallas_call | solution.py:687
Async XLA Ops:
  139.3 3.7 %copy-start = (f32[1536,1536]{1,0:T(8,128)}, f32[1536,1536]{1,0:T(8,128)S(1)}, u32[]{:S(2)}) copy-start(f32[1536,1536]{1,0:T(8,128)S(1)} %get-tuple-element.18.g_up) | copy-start | bytes 28311556
  143.1 3.6 %copy-start.2 = (f32[1536,1536]{1,0:T(8,128)}, f32[1536,1536]{1,0:T(8,128)S(1)}, u32[]{:S(2)}) copy-start(f32[1536,1536]{1,0:T(8,128)S(1)} %get-tuple-element.19.g_down) | copy-start | bytes 28311556
  146.7 3.7 %copy-start.1 = (f32[1536,1536]{1,0:T(8,128)S(1)}, f32[1536,1536]{1,0:T(8,128)}, u32[]{:S(2)}) copy-start(f32[1536,1536]{1,0:T(8,128)} %copy-done) | copy-start | bytes 28311556

commit v3 on v2

--- a/solution.py
+++ b/solution.py
@@ -173,11 +173,11 @@
 
 def step_kernel(R, C, width, params, xa, xb, go, gain, w_up_hbm, w_down_hbm,
                 g_up, g_down, y, dx, gained, verdict,
-                full, acts, w_up, w_down, gain_row, st_own, st_in, keep, buf, inb, buf_p, inb_p,
-                part, from_sib, zbuf, zin, zbuf_p, zin_p, mine, sq,
+                full, acts, w_up, w_down, gain_row, st_own, st_in, partial, buf, inb, buf_p, inb_p,
+                part, from_sib, zbuf, zin, zmid, zbuf_p, zin_p, zmid_p, mine, sq,
                 back_own, back_in, gp_own, gp_in, tt_own, tt_in, uu_own, uu_in,
                 w_sem, st_s, st_r, s_right, s_left, s_sib, recv, hop_s, hop_r, peak_s, peak_r,
-                g_s, g_r, sib_s, sib_r, z_s, z_r, zp_s, zp_r,
+                g_s, g_r, sib_s, sib_r, z_s, z_r, zp_s, zp_r, zm_r, zmp_r,
                 back_s, back_r, gp_s, gp_r, tt_s, tt_r, uu_s, uu_r):
     row, col = lax.axis_index("row"), lax.axis_index("col")
     chips = R // 2
@@ -193,6 +193,8 @@
     tokens = share * R // C
     wide = w_up.shape[1]
     half = wide // 2
+    quarter = wide // C
+    upper = tokens // 2
     tile = half // 2
     high = chip // 2
 
@@ -287,16 +289,18 @@
             pl.when(jnp.logical_not(ends))(lambda: gather(j, 2))
             pl.when(ends)(lambda: gather(j, 3))
 
-    def hop(j, s, peer):
-        return (send(buf.at[j, s], inb.at[j, s], hop_s.at[j, s], hop_r.at[j, s], peer),
-                send(buf_p.at[j, s], inb_p.at[j, s], peak_s.at[j, s], peak_r.at[j, s], peer))
-
-    def go_hop(j, s, peer):
-        for copy in hop(j, s, peer):
+    def hop(n, s):
+        peer = peer_x if s in (0, 2, 3) else peer_y
+        return (send(buf.at[n, s], inb.at[n, s], hop_s.at[n, s], hop_r.at[n, s], peer),
+                send(buf_p.at[n, s], inb_p.at[n, s], peak_s.at[n, s], peak_r.at[n, s], peer))
+
+    def go_hop(n, s, values):
+        buf[n, s], buf_p[n, s] = encode(values)
+        for copy in hop(n, s):
             copy.start()
 
-    def got_hop(j, s):
-        for copy in hop(j, s, peer_x):
+    def got_hop(n, s):
+        for copy in hop(n, s):
             copy.wait_recv()
 
     def over_tiles(body, size):
@@ -304,20 +308,25 @@
         def _(t):
             body(pl.ds(pl.multiple_of(t * tile, tile), tile))
 
-    def role_of(q):
-        return (q + col) % 2, (q // 2 + col // 2) % 2
+    def item(j, k):
+        return j * chips + k
+
+    def place(j, k):
+        return (3 * k + 2 - j) % 6
+
+    def lanes(owner):
+        return pl.ds(pl.multiple_of(owner * quarter, quarter), quarter)
+
+    low_rows, high_rows = slice(0, upper), slice(upper, 2 * upper)
 
     def product(j, k):
         q = order(k)
         owner = 2 * q + 1 - core
         arrived(block(j, owner), recv.at[j, owner], sib)
-        off_x, off_y = role_of(q)
+        n, at_p = item(j, k), place(j, k)
 
         @pl.loop(0, 2)
         def _(h):
-            now = off_x + h * (off_y - off_x)
-            slot = 2 * (1 - off_y) + h * (1 - 2 * off_x + 2 * off_y)
-            s = 2 * (1 - off_y) + h * (3 - 4 * off_x + 2 * off_y)
             at = pl.ds(pl.multiple_of(h * half, half), half)
             left = full[j, pl.ds(q * tokens, tokens), :]
             if j == 2:
@@ -325,139 +334,169 @@
                                         preferred_element_type=F32)
             else:
                 piece = jnp.dot(left, w_up[:, at], preferred_element_type=F32)
-            place = now * 12 + (1 - now) * (j * 4 + slot)
-            keep[place] = piece
-
-            @pl.when(now == 1)
-            def _():
-                def code(part_of):
-                    buf[j, s, :, part_of], buf_p[j, s, :, part_of] = encode(keep[12, :, part_of])
-
-                over_tiles(code, half)
-                go_hop(j, s, {"row": row, "col": flip_x + h * (flip_y - flip_x)})
+            partial[at_p, :, at] = piece
+
+        go_hop(n, 0, partial[at_p, low_rows, lanes(diag)])
+        go_hop(n, 1, partial[at_p, high_rows, lanes(diag)])
+        go_hop(n, 2, partial[at_p, low_rows, lanes(flip_x)])
+        go_hop(n, 5, partial[at_p, high_rows, lanes(flip_y)])
 
     def merge(j, k):
-        off_x, off_y = role_of(order(k))
-
-        @pl.when(off_x + off_y == 1)
-        def _():
-            got_hop(j, off_x)
-
-            def add(at):
-                merged = keep[j * 4 + off_x, :, at] + decode(inb[j, off_x, :, at], inb_p[j, off_x, :, at])
-                buf[j, 4 - off_x, :, at], buf_p[j, 4 - off_x, :, at] = encode(merged)
-
-            over_tiles(add, half)
-            go_hop(j, 4 - off_x, {"row": row, "col": flip_y + off_x * (flip_x - flip_y)})
-
-    def landed(j):
+        n, at_p = item(j, k), place(j, k)
+        got_hop(n, 0)
+        go_hop(n, 4, partial[at_p, low_rows, lanes(flip_y)] + decode(inb[n, 0], inb_p[n, 0]))
+        got_hop(n, 1)
+        go_hop(n, 3, partial[at_p, high_rows, lanes(flip_x)] + decode(inb[n, 1], inb_p[n, 1]))
+
+    def landed(j, k):
         for s in range(2, 6):
-            got_hop(j, s)
-
-    def summed(j, h, at):
-        return (keep[j * 4 + 2 + h, at, :] + decode(inb[j, 2 + h, at, :], inb_p[j, 2 + h])
-                + decode(inb[j, 4 + h, at, :], inb_p[j, 4 + h]))
+            got_hop(item(j, k), s)
+
+    def summed(j, k, r, at, rows):
+        n = item(j, k)
+        first_s, second_s = ((2, 4), (5, 3))[r]
+        return (partial[place(j, k), rows, lanes(col)]
+                + decode(inb[n, first_s, at, :], inb_p[n, first_s])
+                + decode(inb[n, second_s, at, :], inb_p[n, second_s]))
 
     chunk = 16
 
-    def over(body):
-        @pl.loop(0, tokens // chunk)
+    def over(k, body):
+        q = order(k)
+
+        @pl.loop(0, upper // chunk)
         def _(i):
             at = pl.ds(pl.multiple_of(i * chunk, chunk), chunk)
-            to = pl.ds(pl.multiple_of(col * tokens + i * chunk, chunk), chunk)
-            for h in range(2):
-                body(h, at, to, slice(h * half, (h + 1) * half))
-
-    def backward(h, at, to, across):
-        v = summed(1, h, at)
-        phi = 0.5 * (1.0 + lax.erf(v * 0.7071067811865476))
-        g = summed(2, h, at)
-        slope = phi + v * jnp.exp(-0.5 * v * v) * 0.3989422804014327
-        acts[1, to, across] = (v * phi).astype(BF16)
-        acts[2, to, across] = (g * slope).astype(BF16)
-
-    def forward(h, at, to, across):
-        v = summed(0, h, at)
-        acts[0, to, across] = (0.5 * v * (1.0 + lax.erf(v * 0.7071067811865476))).astype(BF16)
-
-    def piece_of(k, owner, h):
-        return acts.at[k, pl.ds(pl.multiple_of(owner * tokens, tokens), tokens), pl.ds(h * half, half)]
-
-    def passing(k, i):
-        owner, h, peer = ((col, 0, peer_x), (col, 1, peer_y), (col, 1, peer_x), (col, 0, peer_y),
+            for r in range(2):
+                rows = pl.ds(pl.multiple_of(r * upper + i * chunk, chunk), chunk)
+                to = pl.ds(pl.multiple_of(q * tokens + r * upper + i * chunk, chunk), chunk)
+                body(r, at, rows, to)
+
+    def backward(k):
+        landed(2, k)
+        landed(1, k)
+
+        def body(r, at, rows, to):
+            v = summed(1, k, r, at, rows)
+            phi = 0.5 * (1.0 + lax.erf(v * 0.7071067811865476))
+            g = summed(2, k, r, at, rows)
+            slope = phi + v * jnp.exp(-0.5 * v * v) * 0.3989422804014327
+            acts[1, to, lanes(col)] = (v * phi).astype(BF16)
+            acts[2, to, lanes(col)] = (g * slope).astype(BF16)
+
+        over(k, body)
+        publish(2, k)
+        publish(1, k)
+
+    def forward(k):
+        landed(0, k)
+
+        def body(r, at, rows, to):
+            v = summed(0, k, r, at, rows)
+            acts[0, to, lanes(col)] = (0.5 * v * (1.0 + lax.erf(v * 0.7071067811865476))).astype(BF16)
+
+        over(k, body)
+        publish(0, k)
+
+    def piece_of(j, k, r, owner):
+        rows = pl.ds(pl.multiple_of(order(k) * tokens + r * upper, upper), upper)
+        return acts.at[j, rows, lanes(owner)]
+
+    def passing(j, k, i):
+        owner, r, peer = ((col, 0, peer_x), (col, 1, peer_y), (col, 1, peer_x), (col, 0, peer_y),
                           (flip_x, 0, peer_y), (flip_y, 1, peer_x))[i]
-        ref = piece_of(k, owner, h)
-        return send(ref, ref, g_s.at[k, i], g_r.at[k, i], peer)
-
-    def publish(k):
+        ref, n = piece_of(j, k, r, owner), item(j, k)
+        return send(ref, ref, g_s.at[n, i], g_r.at[n, i], peer)
+
+    def publish(j, k):
         for i in range(4):
-            passing(k, i).start()
-
-    def pass_on(k):
-        arrived(piece_of(k, flip_x, 0), g_r.at[k, 0], peer_x)
-        passing(k, 4).start()
-        arrived(piece_of(k, flip_y, 1), g_r.at[k, 1], peer_y)
-        passing(k, 5).start()
-
-    def sides(k):
-        arrived(piece_of(k, flip_x, 1), g_r.at[k, 2], peer_x)
-        arrived(piece_of(k, flip_y, 0), g_r.at[k, 3], peer_y)
-
-    def corner(k):
-        arrived(piece_of(k, diag, 0), g_r.at[k, 4], peer_y)
-        arrived(piece_of(k, diag, 1), g_r.at[k, 5], peer_x)
-
-    roles = (col, flip_x, flip_y, diag)
-
-    def to_sib(j, i):
-        return send(part.at[j, i, 1 - core], from_sib.at[j, i], sib_s.at[j, i], sib_r.at[j, i], sib)
-
-    def to_owner(j, i):
-        peer = {"row": 2 * roles[i] + core, "col": col}
-        return (send(zbuf.at[j, i], zin.at[j, chip], z_s.at[j, i], z_r.at[j, chip], peer),
-                send(zbuf_p.at[j, i], zin_p.at[j, chip], zp_s.at[j, i], zp_r.at[j, chip], peer))
-
-    def second(j, i):
+            passing(j, k, i).start()
+
+    def got_piece(j, k, i):
+        owner, r = ((flip_x, 0), (flip_y, 1), (flip_x, 1), (flip_y, 0), (diag, 0), (diag, 1))[i]
+        arrived(piece_of(j, k, r, owner), g_r.at[item(j, k), i], peer_x)
+
+    def pass_on(j, k):
+        got_piece(j, k, 0)
+        passing(j, k, 4).start()
+        got_piece(j, k, 1)
+        passing(j, k, 5).start()
+
+    def complete(j, k):
+        for i in range(2, 6):
+            got_piece(j, k, i)
+
+    def to_sib(j, k):
+        return send(part.at[j, k, 1 - core], from_sib.at[j, k], sib_s.at[j, k], sib_r.at[j, k], sib)
+
+    def to_owner(j, k, h):
+        peer, slot = {"row": 2 * order(k) + core, "col": col}, min(k, 2) - 1
+        return (send(zbuf.at[j, k, h], zin.at[j, slot, h], z_s.at[j, k, h], z_r.at[j, slot, h], peer),
+                send(zbuf_p.at[j, k, h], zin_p.at[j, slot, h], zp_s.at[j, k, h], zp_r.at[j, slot, h], peer))
+
+    def to_middle(j, k, h):
+        peer = {"row": row + 2 - 4 * high, "col": col}
+        return (send(zbuf.at[j, k, h], zmid.at[j, k - 2, h], z_s.at[j, k, h], zm_r.at[j, k - 2, h], peer),
+                send(zbuf_p.at[j, k, h], zmid_p.at[j, k - 2, h], zp_s.at[j, k, h], zmp_r.at[j, k - 2, h], peer))
+
+    def second(j, k):
         @pl.loop(0, 2)
         def _(h):
             at = pl.ds(pl.multiple_of(h * half, half), half)
-            left = acts[2 * j, pl.ds(pl.multiple_of(roles[i] * tokens, tokens), tokens), :]
+            left = acts[2 * j, pl.ds(pl.multiple_of(order(k) * tokens, tokens), tokens), :]
             if j == 0:
                 piece = jnp.dot(left, w_down[:, at], preferred_element_type=F32)
             else:
                 piece = lax.dot_general(left, w_up[at, :], (((1,), (1,)), ((), ())),
                                         preferred_element_type=F32)
-            part[j, i, 0, :, at] = piece[:share]
-            part[j, i, 1, :, at] = piece[share:]
-
-        to_sib(j, i).start()
-
-    def onward(j, i):
-        to_sib(j, i).wait_recv()
-        away = roles[i] != chip
-
-        @pl.when(away)
+            part[j, k, 0, :, at] = piece[:share]
+            part[j, k, 1, :, at] = piece[share:]
+
+        to_sib(j, k).start()
+
+    def in_half(h, at):
+        return pl.ds(pl.multiple_of(h * half + at * tile, tile), tile)
+
+    def code(j, k, h, more, copies):
+        @pl.loop(0, half // tile)
+        def _(t):
+            at, wide_at = pl.ds(pl.multiple_of(t * tile, tile), tile), in_half(h, t)
+            values = part[j, k, core, :, wide_at] + from_sib[j, k, :, wide_at]
+            if more:
+                values = values + decode(zmid[j, k - 2, h, :, at], zmid_p[j, k - 2, h, :, at])
+            zbuf[j, k, h, :, at], zbuf_p[j, k, h, :, at] = encode(values)
+
+        for copy in copies:
+            copy.start()
+
+    def onward(j, k):
+        to_sib(j, k).wait_recv()
+        if k == 0:
+            mine[j] = part[j, k, core] + from_sib[j, k]
+        elif k == 1:
+            for h in range(2):
+                code(j, k, h, False, to_owner(j, k, h))
+        else:
+            @pl.when(ends)
+            def _():
+                for h in range(2):
+                    code(j, k, h, False, to_middle(j, k, h))
+
+    def join(j, k):
+        @pl.when(jnp.logical_not(ends))
         def _():
-            def code(at):
-                zbuf[j, i, :, at], zbuf_p[j, i, :, at] = encode(
-                    part[j, i, core, :, at] + from_sib[j, i, :, at])
-
-            over_tiles(code, columns)
-            for copy in to_owner(j, i):
-                copy.start()
-
-        @pl.when(jnp.logical_not(away))
-        def _():
-            mine[j] = part[j, i, core] + from_sib[j, i]
+            for h in range(2):
+                for copy in to_middle(j, k, h):
+                    copy.wait_recv()
+                code(j, k, h, True, to_owner(j, k, h))
 
     def collect(j):
-        for z in range(chips):
-            @pl.when(z != chip)
-            def _():
-                peer = {"row": 2 * z + core, "col": col}
-                arrived(zin.at[j, z], z_r.at[j, z], peer)
-                arrived(zin_p.at[j, z], zp_r.at[j, z], peer)
-                mine[j] = mine[j] + decode(zin[j, z], zin_p[j, z])
+        for slot in range(2):
+            for h in range(2):
+                for copy in to_owner(j, slot + 1, h):
+                    copy.wait_recv()
+                across = slice(h * half, (h + 1) * half)
+                mine[j, :, across] = mine[j, :, across] + decode(zin[j, slot, h], zin_p[j, slot, h])
 
     def gradient(out, left, right):
         step_m, step_n = 256, half
@@ -474,7 +513,6 @@
 
     load_down.wait()
     product(2, 0)
-    gather_for(2, 1)
     for copy in st_copies:
         copy.wait()
     stats = st_own[...]
@@ -484,75 +522,96 @@
         hat, _ = normal_of(x[...].astype(F32), stats, at, width)
         block(j, row)[...] = (hat * gain_row[...]).astype(BF16)
         mine_of[j] = spread(j, row, 0, block(j, row), True, True)
-        if j == 1:
-            start(mine_of[1])
+        start(mine_of[j])
+    load_up.wait()
+    product(1, 0)
+    merge(2, 0)
+    product(0, 0)
+    merge(1, 0)
+    gather_for(2, 1)
     product(2, 1)
-    merge(2, 0)
+    merge(0, 0)
+    backward(0)
+    gather_for(1, 1)
+    product(1, 1)
+    merge(2, 1)
+    forward(0)
+    gather_for(0, 1)
+    product(0, 1)
+    merge(1, 1)
+    pass_on(2, 0)
+    pass_on(1, 0)
     gather_for(2, 2)
     product(2, 2)
-    merge(2, 1)
-    gather_for(2, 3)
-    start(mine_of[0])
-    load_up.wait()
-    product(2, 3)
-    merge(2, 2)
-    product(1, 0)
-    gather_for(1, 1)
-    merge(2, 3)
-    product(1, 1)
-    merge(1, 0)
+    merge(0, 1)
+    backward(1)
+    pass_on(0, 0)
     gather_for(1, 2)
     product(1, 2)
-    merge(1, 1)
-    gather_for(1, 3)
-    product(1, 3)
-    merge(1, 2)
-    product(0, 0)
-    gather_for(0, 1)
-    merge(1, 3)
-    landed(2)
-    landed(1)
-    over(backward)
-    publish(2)
-    publish(1)
-    product(0, 1)
-    merge(0, 0)
+    merge(2, 2)
+    forward(1)
+    complete(2, 0)
     second(1, 0)
     gather_for(0, 2)
     product(0, 2)
-    merge(0, 1)
-    pass_on(2)
+    merge(1, 2)
+    pass_on(2, 1)
+    pass_on(1, 1)
+    complete(0, 0)
+    second(0, 0)
+    onward(1, 0)
+    gather_for(2, 3)
+    product(2, 3)
+    merge(0, 2)
+    backward(2)
+    pass_on(0, 1)
+    gather_for(1, 3)
+    product(1, 3)
+    merge(2, 3)
+    forward(2)
+    complete(2, 1)
+    second(1, 1)
     gather_for(0, 3)
     product(0, 3)
-    merge(0, 2)
-    onward(1, 0)
-    sides(2)
-    second(1, 1)
+    merge(1, 3)
+    onward(0, 0)
+    pass_on(2, 2)
+    pass_on(1, 2)
+    complete(0, 1)
+    second(0, 1)
+    onward(1, 1)
     merge(0, 3)
+    backward(3)
+    pass_on(0, 2)
+    forward(3)
+    complete(2, 2)
     second(1, 2)
-    pass_on(1)
-    landed(0)
-    over(forward)
-    publish(0)
-    onward(1, 1)
+    onward(0, 1)
+    pass_on(2, 3)
+    pass_on(1, 3)
     onward(1, 2)
-    corner(2)
+    complete(0, 2)
+    second(0, 2)
+    pass_on(0, 3)
+    onward(0, 2)
+    complete(2, 3)
     second(1, 3)
-    second(0, 0)
+    join(1, 2)
     onward(1, 3)
+    complete(0, 3)
+    second(0, 3)
+    join(0, 2)
+    onward(0, 3)
     gradient(g_up, full.at[1], acts.at[2])
-    onward(0, 0)
-    sides(1)
-    corner(1)
-    pass_on(0)
+    join(1, 3)
+    for k in range(chips):
+        complete(1, k)
     gradient(g_down, acts.at[1], full.at[2])
+    join(0, 3)
     tt_own[...] = jnp.broadcast_to(jnp.sum(sq[...], 1, keepdims=True), tt_own.shape)
     third = [send(tt_own, tt_in.at[row], tt_s.at[i], tt_r.at[i], p) for i, p in enumerate(rows_of)]
     for copy in third:
         copy.start()
-    sides(0)
-    second(0, 1)
-    second(0, 2)
     collect(1)
     grad = mine[1]
     hat, inv = normal_of(xb[...].astype(F32), stats, 2, width)
@@ -567,15 +626,10 @@
     gains_out = [send(gp_own, gp_in.at[row], gp_s.at[i], gp_r.at[i], p) for i, p in enumerate(rows_of)]
     for copy in gains_out:
         copy.start()
-    onward(0, 1)
-    onward(0, 2)
-    corner(0)
-    second(0, 3)
     gp_in[row] = gp_own[...]
     tt_in[row] = tt_own[...]
     for copy in gains_out + third:
         copy.wait()
-    onward(0, 3)
     gains, squares = gp_in[0], tt_in[0]
     for i in range(1, R):
         gains, squares = gains + gp_in[i], squares + tt_in[i]
@@ -608,18 +662,21 @@
     for j in (2, 1, 0):
         finish(mine_of[j])
         relays(j, lambda owner, sign, copies: finish(copies), range(1, chips))
-        for i in range(6):
-            passing(j, i).wait_send()
-            for copy in hop(j, i, peer_x):
-                copy.wait_send()
+        for k in range(chips):
+            for i in range(6):
+                passing(j, k, i).wait_send()
+                for copy in hop(item(j, k), i):
+                    copy.wait_send()
     for j in (0, 1):
         for i in range(chips):
             to_sib(j, i).wait_send()
-
-            @pl.when(roles[i] != chip)
-            def _():
-                for copy in to_owner(j, i):
-                    copy.wait_send()
+            for h in range(2):
+                if i == 1:
+                    for copy in to_owner(j, i, h):
+                        copy.wait_send()
+                elif i > 1:
+                    for copy in to_middle(j, i, h):
+                        copy.wait_send()
 
 
 def step_on_core(R, C, width, params, x_fwd, x_bwd, grad_out, gain, w_up, w_down):
@@ -640,12 +697,13 @@
             VM((3, count, columns), BF16), VM((3, count, wide), BF16),
             VM(w_up.shape, BF16), VM(w_down.shape, BF16), VM((1, columns), F32),
             VM((rows, 128), F32), VM((C - 1, rows, 128), F32),
-            VM((13, tokens, half), F32),
-            VM((3, 6, tokens, half), BF16), VM((3, 6, tokens, half), BF16),
-            VM((3, 6, 1, half), F32), VM((3, 6, 1, half), F32),
+            VM((6, tokens, wide), F32),
+            VM((12, 6, tokens // 2, wide // C), BF16), VM((12, 6, tokens // 2, wide // C), BF16),
+            VM((12, 6, 1, wide // C), F32), VM((12, 6, 1, wide // C), F32),
             VM((2, chips, 2, rows, columns), F32), VM((2, chips, rows, columns), F32),
-            VM((2, chips, rows, columns), BF16), VM((2, chips, rows, columns), BF16),
-            VM((2, chips, 1, columns), F32), VM((2, chips, 1, columns), F32),
+            VM((2, chips, 2, rows, half), BF16), VM((2, 2, 2, rows, half), BF16),
+            VM((2, 2, 2, rows, half), BF16), VM((2, chips, 2, 1, half), F32),
+            VM((2, 2, 2, 1, half), F32), VM((2, 2, 2, 1, half), F32),
             VM((2, rows, columns), F32), VM((1, columns), F32),
             VM((rows, 128), F32), VM((C - 1, rows, 128), F32),
             VM((lines, 128), F32), VM((R, lines, 128), F32),
@@ -653,7 +711,8 @@
         ]
         + [DMA((2,)), DMA((C - 1,)), DMA((C - 1,)),
            DMA((3, slots)), DMA((3, slots)), DMA((3, slots)), DMA((3, R))]
-        + [DMA((3, 6))] * 6 + [DMA((2, chips))] * 6
+        + [DMA((12, 6))] * 6 + [DMA((2, chips))] * 2
+        + [DMA((2, chips, 2)), DMA((2, 2, 2))] * 2 + [DMA((2, 2, 2))] * 2
         + [DMA((C - 1,))] * 2 + [DMA((R - 1,))] * 4 + [DMA((C - 1,))] * 2,
         compiler_params=pltpu.CompilerParams(
             collective_id=0, has_side_effects=True, vmem_limit_bytes=GRANT),
@@ -691,9 +750,9 @@
         in_specs=[VMEM] * 6,
         out_specs=(pl.BlockSpec(memory_space=pl.ANY),) * 2 + (VMEM,) * 4,
         scratch_shapes=[pltpu.VMEM((2, slots, size, g_up.shape[1]), F32), DMA((2, slots))],
-        compiler_params=pltpu.CompilerParams(vmem_limit_bytes=40 * 1024 * 1024),
+        compiler_params=pltpu.CompilerParams(vmem_limit_bytes=20 * 1024 * 1024),
         cost_estimate=pl.CostEstimate(flops=10**8, bytes_accessed=4 * 10**7, transcendentals=0),
-    )(g_up, g_down, y, dx, gains, verdict)
+    )(*(pltpu.with_memory_space_constraint(v, pltpu.VMEM) for v in (g_up, g_down, y, dx, gains, verdict)))
 
 
 def with_kernels(R, C):

time: 162 us -> 132 us (0.81)
  the two profiles are of different devices: /device:TPU:24 before, /device:TPU:0 now
where the time goes in v3:
time: 132 us
  Pallas kernels  131 us (99%)
    pallas_call x1, Pallas kernels, step_on_core(): pl.pallas_call(functools.partial(step_kernel, R, C, width, params), out_s...  124 us
    pallas_call x1, Pallas kernels, clip(): pl.pallas_call(clip_kernel, out_shape=(like(g_up.shape, F32), like(g_down...  7.5 us

profile of v3, /device:TPU:0, one launch (start us, length us, event | category | flops | bytes accessed | tf_op | source)
XLA Modules:
  0.0 132.2 jit_solution(13172079281660070025)
XLA Ops:
  0.6 123.9 %shard_map.109 = (f32[1536,1536]{1,0:T(8,128)S(1)}, f32[1536,1536]{1,0:T(8,128)S(1)}, bf16[64,1536]{1,0:T(8,128)(2,1)S(1)}, bf16[64,1536]{1,0:T(8,128)(2,1)S(1)}...) custom-call(bf16[64,1536]{1,0:T(8,128)(2,1)} %xa.1, bf16[64,1536]{1,0:T(8,128)(2,1)} %xb.1, bf16[64,1536]{1,0:T(8,128)(2,1)} %go.1, ...), custom_call_target="tpu_custom_call" | custom-call | flops 20000000000 | bytes 10000000 | tf_op jit(solution)/shard_map/pallas_call | solution.py:690
  124.6 7.5 %shard_map.110 = (f32[1536,1536]{1,0:T(8,128)}, f32[1536,1536]{1,0:T(8,128)}, bf16[64,1536]{1,0:T(8,128)(2,1)}, bf16[64,1536]{1,0:T(8,128)(2,1)}, f32[12,128]{1,0:T(8,128)}, /*index=5*/f32[1,1]{1,0:T(1,128)}) custom-call(f32[1536,1536]{1,0:T(8,128)S(1)} %get-tuple-element.18.g_up, f32[1536,1536]{1,0:T(8,128)S(1)} %get-tuple-element.19.g_down, ...), custom_call_target="tpu_custom_call" | custom-call | flops 100000000 | bytes 40000000 | tf_op jit(solution)/shard_map/pallas_call | solution.py:746

commit v4 on v3

--- a/solution.py
+++ b/solution.py
@@ -175,10 +175,10 @@
                 g_up, g_down, y, dx, gained, verdict,
                 full, acts, w_up, w_down, gain_row, st_own, st_in, partial, buf, inb, buf_p, inb_p,
                 part, from_sib, zbuf, zin, zmid, zbuf_p, zin_p, zmid_p, mine, sq,
-                back_own, back_in, gp_own, gp_in, tt_own, tt_in, uu_own, uu_in,
+                back_own, back_in, gp_own, gp_in, uu_own, uu_in,
                 w_sem, st_s, st_r, s_right, s_left, s_sib, recv, hop_s, hop_r, peak_s, peak_r,
                 g_s, g_r, sib_s, sib_r, z_s, z_r, zp_s, zp_r, zm_r, zmp_r,
-                back_s, back_r, gp_s, gp_r, tt_s, tt_r, uu_s, uu_r):
+                back_s, back_r, gp_s, gp_r, uu_s, uu_r):
     row, col = lax.axis_index("row"), lax.axis_index("col")
     chips = R // 2
     chip, core = row // 2, row % 2
@@ -281,12 +281,9 @@
     ends = (chip + 1) % chips < 2
 
     def gather_for(j, k):
-        if k == 1:
-            gather(j, 1)
-        elif k == 2:
-            pl.when(ends)(lambda: gather(j, 2))
-        elif k == 3:
-            pl.when(jnp.logical_not(ends))(lambda: gather(j, 2))
+        if k < 3:
+            gather(j, k)
+        else:
             pl.when(ends)(lambda: gather(j, 3))
 
     def hop(n, s):
@@ -312,7 +309,7 @@
         return j * chips + k
 
     def place(j, k):
-        return (3 * k + 2 - j) % 6
+        return 4 + k % 2 if j == 0 else (2 * k + 2 - j) % 4
 
     def lanes(owner):
         return pl.ds(pl.multiple_of(owner * quarter, quarter), quarter)
@@ -498,10 +495,11 @@
                 across = slice(h * half, (h + 1) * half)
                 mine[j, :, across] = mine[j, :, across] + decode(zin[j, slot, h], zin_p[j, slot, h])
 
-    def gradient(out, left, right):
+    def gradient(out, left, right, part_of):
         step_m, step_n = 256, half
-
-        @pl.loop(0, out.shape[0] // step_m)
+        blocks = out.shape[0] // step_m // 2
+
+        @pl.loop(part_of * blocks, (part_of + 1) * blocks)
         def _(m):
             at = pl.ds(pl.multiple_of(m * step_m, step_m), step_m)
             for n in range(out.shape[1] // step_n):
@@ -530,88 +528,81 @@
     merge(1, 0)
     gather_for(2, 1)
     product(2, 1)
-    merge(0, 0)
     backward(0)
     gather_for(1, 1)
     product(1, 1)
     merge(2, 1)
-    forward(0)
     gather_for(0, 1)
-    product(0, 1)
-    merge(1, 1)
+    merge(0, 0)
     pass_on(2, 0)
     pass_on(1, 0)
+    merge(1, 1)
     gather_for(2, 2)
+    forward(0)
+    gather_for(1, 2)
     product(2, 2)
-    merge(0, 1)
     backward(1)
-    pass_on(0, 0)
-    gather_for(1, 2)
     product(1, 2)
     merge(2, 2)
-    forward(1)
     complete(2, 0)
     second(1, 0)
     gather_for(0, 2)
-    product(0, 2)
-    merge(1, 2)
+    pass_on(0, 0)
     pass_on(2, 1)
     pass_on(1, 1)
-    complete(0, 0)
-    second(0, 0)
-    onward(1, 0)
+    merge(1, 2)
     gather_for(2, 3)
     product(2, 3)
-    merge(0, 2)
     backward(2)
-    pass_on(0, 1)
+    onward(1, 0)
     gather_for(1, 3)
     product(1, 3)
     merge(2, 3)
-    forward(2)
+    product(0, 1)
     complete(2, 1)
     second(1, 1)
-    gather_for(0, 3)
-    product(0, 3)
     merge(1, 3)
-    onward(0, 0)
     pass_on(2, 2)
     pass_on(1, 2)
-    complete(0, 1)
-    second(0, 1)
+    merge(0, 1)
     onward(1, 1)
-    merge(0, 3)
+    complete(0, 0)
+    second(0, 0)
     backward(3)
-    pass_on(0, 2)
-    forward(3)
+    onward(0, 0)
     complete(2, 2)
     second(1, 2)
-    onward(0, 1)
     pass_on(2, 3)
+    onward(1, 2)
+    forward(1)
     pass_on(1, 3)
-    onward(1, 2)
-    complete(0, 2)
-    second(0, 2)
-    pass_on(0, 3)
-    onward(0, 2)
+    product(0, 2)
+    gather_for(0, 3)
     complete(2, 3)
     second(1, 3)
+    pass_on(0, 1)
+    product(0, 3)
+    onward(1, 3)
+    merge(0, 2)
     join(1, 2)
-    onward(1, 3)
-    complete(0, 3)
-    second(0, 3)
-    join(0, 2)
-    onward(0, 3)
-    gradient(g_up, full.at[1], acts.at[2])
+    gradient(g_up, full.at[1], acts.at[2], 0)
+    merge(0, 3)
+    forward(2)
+    gradient(g_up, full.at[1], acts.at[2], 1)
     join(1, 3)
     for k in range(chips):
         complete(1, k)
-    gradient(g_down, acts.at[1], full.at[2])
-    join(0, 3)
-    tt_own[...] = jnp.broadcast_to(jnp.sum(sq[...], 1, keepdims=True), tt_own.shape)
-    third = [send(tt_own, tt_in.at[row], tt_s.at[i], tt_r.at[i], p) for i, p in enumerate(rows_of)]
-    for copy in third:
-        copy.start()
+    gradient(g_down, acts.at[1], full.at[2], 0)
+    pass_on(0, 2)
+    forward(3)
+    complete(0, 1)
+    second(0, 1)
+    complete(0, 2)
+    second(0, 2)
+    onward(0, 1)
+    pass_on(0, 3)
+    onward(0, 2)
+    gradient(g_down, acts.at[1], full.at[2], 1)
     collect(1)
     grad = mine[1]
     hat, inv = normal_of(xb[...].astype(F32), stats, 2, width)
@@ -620,25 +611,31 @@
     first = [send(back_own, back_in.at[i], back_s.at[i], back_r.at[i], p) for i, p in enumerate(cols)]
     for copy in first:
         copy.start()
+    lines = columns // 128
     gain_part = jnp.sum(grad * hat, 0, keepdims=True)
-    for i in range(columns // 128):
+    for i in range(lines):
         gp_own[i : i + 1, :] = gain_part[:, i * 128 : (i + 1) * 128]
+    gp_own[lines : lines + 1, :] = jnp.broadcast_to(jnp.sum(sq[...], 1, keepdims=True), (1, 128))
     gains_out = [send(gp_own, gp_in.at[row], gp_s.at[i], gp_r.at[i], p) for i, p in enumerate(rows_of)]
     for copy in gains_out:
         copy.start()
     gp_in[row] = gp_own[...]
-    tt_in[row] = tt_own[...]
-    for copy in gains_out + third:
+    complete(0, 3)
+    second(0, 3)
+    onward(0, 3)
+    join(0, 2)
+    for copy in gains_out:
         copy.wait()
-    gains, squares = gp_in[0], tt_in[0]
+    gains = gp_in[0]
     for i in range(1, R):
-        gains, squares = gains + gp_in[i], squares + tt_in[i]
-    gained[...] = gains
-    uu_own[...] = squares + jnp.sum(gains * gains)
+        gains = gains + gp_in[i]
+    gained[...] = gains[:lines]
+    uu_own[...] = jnp.broadcast_to(gains[lines : lines + 1], (8, 128)) + jnp.sum(gains[:lines] * gains[:lines])
     fourth = [send(uu_own, uu_in.at[col], uu_s.at[i], uu_r.at[i], p) for i, p in enumerate(cols)]
     for copy in fourth:
         copy.start()
     uu_in[col] = uu_own[...]
+    join(0, 3)
     for copy in first:
         copy.wait()
     sums = back_own[...]
@@ -706,14 +703,14 @@
             VM((2, 2, 2, 1, half), F32), VM((2, 2, 2, 1, half), F32),
             VM((2, rows, columns), F32), VM((1, columns), F32),
             VM((rows, 128), F32), VM((C - 1, rows, 128), F32),
-            VM((lines, 128), F32), VM((R, lines, 128), F32),
-            VM((8, 128), F32), VM((R, 8, 128), F32), VM((8, 128), F32), VM((C, 8, 128), F32),
+            VM((lines + 1, 128), F32), VM((R, lines + 1, 128), F32),
+            VM((8, 128), F32), VM((C, 8, 128), F32),
         ]
         + [DMA((2,)), DMA((C - 1,)), DMA((C - 1,)),
            DMA((3, slots)), DMA((3, slots)), DMA((3, slots)), DMA((3, R))]
         + [DMA((12, 6))] * 6 + [DMA((2, chips))] * 2
         + [DMA((2, chips, 2)), DMA((2, 2, 2))] * 2 + [DMA((2, 2, 2))] * 2
-        + [DMA((C - 1,))] * 2 + [DMA((R - 1,))] * 4 + [DMA((C - 1,))] * 2,
+        + [DMA((C - 1,))] * 2 + [DMA((R - 1,))] * 2 + [DMA((C - 1,))] * 2,
         compiler_params=pltpu.CompilerParams(
             collective_id=0, has_side_effects=True, vmem_limit_bytes=GRANT),
         cost_estimate=pl.CostEstimate(flops=2 * 10**10, bytes_accessed=10**7, transcendentals=0),

time: 132 us -> 125 us (0.947)
  Pallas kernels: 131 us -> 124 us
    pallas_call x1, Pallas kernels: 124 us -> 117 us  [step_on_core(): pl.pallas_call(functools.partial(step_kernel, R, C, width, params), out_s...]
where the time goes in v4:
time: 125 us
  Pallas kernels  124 us (99%)
    pallas_call x1, Pallas kernels, step_on_core(): pl.pallas_call(functools.partial(step_kernel, R, C, width, params), out_s...  117 us
    pallas_call x1, Pallas kernels, clip(): pl.pallas_call(clip_kernel, out_shape=(like(g_up.shape, F32), like(g_down...  7.5 us

profile of v4, /device:TPU:0, one launch (start us, length us, event | category | flops | bytes accessed | tf_op | source)
XLA Modules:
  0.0 125.0 jit_solution(1736351614535466258)
XLA Ops:
  0.6 116.7 %shard_map.109 = (f32[1536,1536]{1,0:T(8,128)S(1)}, f32[1536,1536]{1,0:T(8,128)S(1)}, bf16[64,1536]{1,0:T(8,128)(2,1)S(1)}, bf16[64,1536]{1,0:T(8,128)(2,1)S(1)}...) custom-call(bf16[64,1536]{1,0:T(8,128)(2,1)} %xa.1, bf16[64,1536]{1,0:T(8,128)(2,1)} %xb.1, bf16[64,1536]{1,0:T(8,128)(2,1)} %go.1, ...), custom_call_target="tpu_custom_call" | custom-call | flops 20000000000 | bytes 10000000 | tf_op jit(solution)/shard_map/pallas_call | solution.py:687
  117.3 7.5 %shard_map.110 = (f32[1536,1536]{1,0:T(8,128)}, f32[1536,1536]{1,0:T(8,128)}, bf16[64,1536]{1,0:T(8,128)(2,1)}, bf16[64,1536]{1,0:T(8,128)(2,1)}, f32[12,128]{1,0:T(8,128)}, /*index=5*/f32[1,1]{1,0:T(1,128)}) custom-call(f32[1536,1536]{1,0:T(8,128)S(1)} %get-tuple-element.18.g_up, f32[1536,1536]{1,0:T(8,128)S(1)} %get-tuple-element.19.g_down, ...), custom_call_target="tpu_custom_call" | custom-call | flops 100000000 | bytes 40000000 | tf_op jit(solution)/shard_map/pallas_call | solution.py:743

commit v5 on v4

--- a/solution.py
+++ b/solution.py
@@ -495,19 +495,23 @@
                 across = slice(h * half, (h + 1) * half)
                 mine[j, :, across] = mine[j, :, across] + decode(zin[j, slot, h], zin_p[j, slot, h])
 
-    def gradient(out, left, right, part_of):
+    def gradient(out, left, right, late):
         step_m, step_n = 256, half
-        blocks = out.shape[0] // step_m // 2
-
-        @pl.loop(part_of * blocks, (part_of + 1) * blocks)
+        depth = 2 * tokens
+        from_row = (high + late * (1 - 2 * high)) * depth
+        rows = pl.ds(pl.multiple_of(from_row, depth), depth)
+
+        @pl.loop(0, out.shape[0] // step_m)
         def _(m):
             at = pl.ds(pl.multiple_of(m * step_m, step_m), step_m)
             for n in range(out.shape[1] // step_n):
                 across = slice(n * step_n, (n + 1) * step_n)
-                piece = lax.dot_general(left[:, at], right[:, across], (((0,), (0,)), ((), ())),
+                piece = lax.dot_general(left[rows, at], right[rows, across], (((0,), (0,)), ((), ())),
                                         preferred_element_type=F32)
+                if late:
+                    piece = piece + out[at, across]
+                    sq[:, across] = sq[:, across] + jnp.sum(piece * piece, 0, keepdims=True)
                 out[at, across] = piece
-                sq[:, across] = sq[:, across] + jnp.sum(piece * piece, 0, keepdims=True)
 
     load_down.wait()
     product(2, 0)
@@ -553,18 +557,23 @@
     merge(1, 2)
     gather_for(2, 3)
     product(2, 3)
+    complete(2, 1)
+    gradient(g_up, full.at[1], acts.at[2], 0)
     backward(2)
     onward(1, 0)
     gather_for(1, 3)
     product(1, 3)
     merge(2, 3)
-    product(0, 1)
-    complete(2, 1)
+    gather_for(0, 3)
+    product(0, 3)
     second(1, 1)
     merge(1, 3)
     pass_on(2, 2)
     pass_on(1, 2)
-    merge(0, 1)
+    complete(1, 0)
+    complete(1, 1)
+    gradient(g_down, acts.at[1], full.at[2], 0)
+    merge(0, 3)
     onward(1, 1)
     complete(0, 0)
     second(0, 0)
@@ -574,35 +583,33 @@
     second(1, 2)
     pass_on(2, 3)
     onward(1, 2)
-    forward(1)
+    forward(3)
     pass_on(1, 3)
     product(0, 2)
-    gather_for(0, 3)
     complete(2, 3)
     second(1, 3)
-    pass_on(0, 1)
-    product(0, 3)
+    pass_on(0, 3)
+    product(0, 1)
     onward(1, 3)
     merge(0, 2)
     join(1, 2)
-    gradient(g_up, full.at[1], acts.at[2], 0)
-    merge(0, 3)
+    gradient(g_up, full.at[1], acts.at[2], 1)
+    complete(0, 3)
+    second(0, 3)
+    merge(0, 1)
     forward(2)
-    gradient(g_up, full.at[1], acts.at[2], 1)
+    onward(0, 3)
     join(1, 3)
-    for k in range(chips):
-        complete(1, k)
-    gradient(g_down, acts.at[1], full.at[2], 0)
+    complete(1, 2)
+    complete(1, 3)
+    gradient(g_down, acts.at[1], full.at[2], 1)
     pass_on(0, 2)
-    forward(3)
-    complete(0, 1)
-    second(0, 1)
+    forward(1)
+    join(0, 3)
     complete(0, 2)
     second(0, 2)
-    onward(0, 1)
-    pass_on(0, 3)
+    pass_on(0, 1)
     onward(0, 2)
-    gradient(g_down, acts.at[1], full.at[2], 1)
     collect(1)
     grad = mine[1]
     hat, inv = normal_of(xb[...].astype(F32), stats, 2, width)
@@ -620,9 +627,9 @@
     for copy in gains_out:
         copy.start()
     gp_in[row] = gp_own[...]
-    complete(0, 3)
-    second(0, 3)
-    onward(0, 3)
+    complete(0, 1)
+    second(0, 1)
+    onward(0, 1)
     join(0, 2)
     for copy in gains_out:
         copy.wait()
@@ -635,7 +642,6 @@
     for copy in fourth:
         copy.start()
     uu_in[col] = uu_own[...]
-    join(0, 3)
     for copy in first:
         copy.wait()
     sums = back_own[...]

time: 125 us -> 118 us (0.944)
  Pallas kernels: 124 us -> 117 us
    pallas_call x1, Pallas kernels: 117 us -> 109 us  [step_on_core(): pl.pallas_call(functools.partial(step_kernel, R, C, width, params), out_s...]
where the time goes in v5:
time: 118 us; the launch traced here: 117 us
  Pallas kernels  117 us (99%)
    pallas_call x1, Pallas kernels, step_on_core(): pl.pallas_call(functools.partial(step_kernel, R, C, width, params), out_s...  109 us
    pallas_call x1, Pallas kernels, clip(): pl.pallas_call(clip_kernel, out_shape=(like(g_up.shape, F32), like(g_down...  7.5 us

profile of v5, /device:TPU:0, one launch (start us, length us, event | category | flops | bytes accessed | tf_op | source)
XLA Modules:
  0.0 117.4 jit_solution(11590732074238481242)
XLA Ops:
  0.6 109.1 %shard_map.109 = (f32[1536,1536]{1,0:T(8,128)S(1)}, f32[1536,1536]{1,0:T(8,128)S(1)}, bf16[64,1536]{1,0:T(8,128)(2,1)S(1)}, bf16[64,1536]{1,0:T(8,128)(2,1)S(1)}...) custom-call(bf16[64,1536]{1,0:T(8,128)(2,1)} %xa.1, bf16[64,1536]{1,0:T(8,128)(2,1)} %xb.1, bf16[64,1536]{1,0:T(8,128)(2,1)} %go.1, ...), custom_call_target="tpu_custom_call" | custom-call | flops 20000000000 | bytes 10000000 | tf_op jit(solution)/shard_map/pallas_call | solution.py:693
  109.8 7.5 %shard_map.110 = (f32[1536,1536]{1,0:T(8,128)}, f32[1536,1536]{1,0:T(8,128)}, bf16[64,1536]{1,0:T(8,128)(2,1)}, bf16[64,1536]{1,0:T(8,128)(2,1)}, f32[12,128]{1,0:T(8,128)}, /*index=5*/f32[1,1]{1,0:T(1,128)}) custom-call(f32[1536,1536]{1,0:T(8,128)S(1)} %get-tuple-element.18.g_up, f32[1536,1536]{1,0:T(8,128)S(1)} %get-tuple-element.19.g_down, ...), custom_call_target="tpu_custom_call" | custom-call | flops 100000000 | bytes 40000000 | tf_op jit(solution)/shard_map/pallas_call | solution.py:749

commit v6 on v5

--- a/solution.py
+++ b/solution.py
@@ -597,19 +597,14 @@
     complete(0, 3)
     second(0, 3)
     merge(0, 1)
+    join(1, 3)
     forward(2)
     onward(0, 3)
-    join(1, 3)
     complete(1, 2)
     complete(1, 3)
     gradient(g_down, acts.at[1], full.at[2], 1)
     pass_on(0, 2)
     forward(1)
-    join(0, 3)
-    complete(0, 2)
-    second(0, 2)
-    pass_on(0, 1)
-    onward(0, 2)
     collect(1)
     grad = mine[1]
     hat, inv = normal_of(xb[...].astype(F32), stats, 2, width)
@@ -627,6 +622,11 @@
     for copy in gains_out:
         copy.start()
     gp_in[row] = gp_own[...]
+    join(0, 3)
+    complete(0, 2)
+    second(0, 2)
+    pass_on(0, 1)
+    onward(0, 2)
     complete(0, 1)
     second(0, 1)
     onward(0, 1)

time: 118 us -> 118 us (level)
  no operation moved by 1% of the time
where the time goes in v6:
time: 118 us; the launch traced here: 117 us
  Pallas kernels  116 us (98%)
    pallas_call x1, Pallas kernels, step_on_core(): pl.pallas_call(functools.partial(step_kernel, R, C, width, params), out_s...  109 us
    pallas_call x1, Pallas kernels, clip(): pl.pallas_call(clip_kernel, out_shape=(like(g_up.shape, F32), like(g_down...  7.5 us

profile of v6, /device:TPU:0, one launch (start us, length us, event | category | flops | bytes accessed | tf_op | source)
XLA Modules:
  0.0 117.1 jit_solution(4107292317629997785)
XLA Ops:
  0.6 108.8 %shard_map.109 = (f32[1536,1536]{1,0:T(8,128)S(1)}, f32[1536,1536]{1,0:T(8,128)S(1)}, bf16[64,1536]{1,0:T(8,128)(2,1)S(1)}, bf16[64,1536]{1,0:T(8,128)(2,1)S(1)}...) custom-call(bf16[64,1536]{1,0:T(8,128)(2,1)} %xa.1, bf16[64,1536]{1,0:T(8,128)(2,1)} %xb.1, bf16[64,1536]{1,0:T(8,128)(2,1)} %go.1, ...), custom_call_target="tpu_custom_call" | custom-call | flops 20000000000 | bytes 10000000 | tf_op jit(solution)/shard_map/pallas_call | solution.py:693
  109.4 7.5 %shard_map.110 = (f32[1536,1536]{1,0:T(8,128)}, f32[1536,1536]{1,0:T(8,128)}, bf16[64,1536]{1,0:T(8,128)(2,1)}, bf16[64,1536]{1,0:T(8,128)(2,1)}, f32[12,128]{1,0:T(8,128)}, /*index=5*/f32[1,1]{1,0:T(1,128)}) custom-call(f32[1536,1536]{1,0:T(8,128)S(1)} %get-tuple-element.18.g_up, f32[1536,1536]{1,0:T(8,128)S(1)} %get-tuple-element.19.g_down, ...), custom_call_target="tpu_custom_call" | custom-call | flops 100000000 | bytes 40000000 | tf_op jit(solution)/shard_map/pallas_call | solution.py:749
